TPU v7x, 256 devices: a whole 4x4x8 slice. The times are simulated.
256 devices in a mesh: section: 16 (over z, x_lo), fsdp: 16 (over x_hi, y, core).
Axes of the slice: x: 4 (x_hi: 2, x_lo: 2; x = x_hi * 2 + x_lo), y: 4, z: 8, core: 2. Of those that a mesh axis runs over, the one named last changes fastest.
Arguments:
- layer_inputs: bfloat16 [16, 2, 6144, 2048], P('section', None, 'fsdp'), may hold values from -6 to 6
- out_grads: bfloat16 [16, 2, 6144, 2048], P('section', None, 'fsdp'), may hold values from -6 to 6
- attn_stash: bfloat16 [16, 2, 6144, 1024], P('section', None, 'fsdp'), may hold values from -6 to 6
- proj_grads: bfloat16 [16, 2, 6144, 1536], P('section', None, 'fsdp'), may hold values from -6 to 6
- w_qkv: bfloat16 [16, 2048, 1536], P('section', 'fsdp'), may hold values from -0.125 to 0.125
- w_out: bfloat16 [16, 1024, 2048], P('section', 'fsdp'), may hold values from -0.1875 to 0.1875
- norm_gain: float32 [16, 2048], P('section'), may hold values from 0.25 to 1.75
- b_sched: int32 [16], P('section'), may hold values from 0 to 1
- w_sched: int32 [16], P('section'), may hold values from 0 to 1
Outputs:
- prev_grads: bfloat16 [16, 6144, 2048], P('section', 'fsdp')
- grad_qkv: float32 [16, 2048, 1536], P('section', 'fsdp')
- grad_out: float32 [16, 1024, 2048], P('section', 'fsdp')
All inputs are finite; a program needn't handle non-finite values.
Results may differ from a plain program's by a relative error of at most 0.012.
Values may be sent and summed in bfloat16 or wider, within the bound.
No kernel may reach another device: no remote copies, remote signals or barrier semaphores. Data moves between devices by JAX's collectives and lax.ppermute only.
A program may use at most 128 MiB of HBM per device.

v0:
```python
import jax
import jax.numpy as jnp
from jax import lax
from jax.experimental import pallas as pl
from jax.experimental.pallas import tpu as pltpu
from jax.sharding import Mesh
from jax.sharding import PartitionSpec as P


HEAD_DIM = 64
KV_HEADS = 4
SECTION = ("z", "x_lo")
FSDP = ("x_hi", "y", "core")
SEQ = 384
D = 2048
QW = 1024
WIDTH = 1536
BLOCK = 512
Q_ROWS = 384
PIECE = 640
TILE = 128


rms_eps = 1e-05
rope_base = 500000.0
f32 = jnp.float32
bf16 = jnp.bfloat16

GROUPS = (((0, 0), (1, 0)), ((0, 1), (0, 3)), ((1, 1), (1, 3)), ((0, 2), (1, 2)))

VMEM = pl.BlockSpec(memory_space=pltpu.VMEM)
SMEM = pl.BlockSpec(memory_space=pltpu.SMEM)
HBM = pl.BlockSpec(memory_space=pltpu.HBM)


def passed_along(array, axis, by):
    size = lax.axis_size(axis)
    return lax.ppermute(array, axis, [(i, (i + by) % size) for i in range(size)])


def from_above(array):
    return passed_along(array, "y", -1)


def from_below(array):
    return passed_along(array, "y", 1)


def limit(mebibytes):
    return pltpu.CompilerParams(vmem_limit_bytes=mebibytes << 20)


def pack_body(qkv, out, packed):
    for j in range(3):
        packed[j * TILE : (j + 1) * TILE, :] = qkv[0, :, j * BLOCK : (j + 1) * BLOCK]
    for j in range(4):
        packed[Q_ROWS + j * HEAD_DIM : Q_ROWS + (j + 1) * HEAD_DIM, :] = out[
            0, :, j * BLOCK : (j + 1) * BLOCK
        ]


def packed_shard(qkv, out):
    return pl.pallas_call(
        pack_body,
        in_specs=[VMEM, VMEM],
        out_specs=VMEM,
        out_shape=jax.ShapeDtypeStruct((PIECE, BLOCK), bf16),
        compiler_params=limit(4),
        name="pack",
    )(qkv, out)


def gathered_groups(shard):
    other = passed_along(shard, "x_hi", 1)
    above, below = (from_above(shard), from_below(shard))
    above_other = from_above(other)
    below_other = from_below(other)
    far = from_above(above)
    far_other = from_below(below_other)

    def with_peer(array):
        return (array, passed_along(array, "core", 1))

    return (
        (*with_peer(shard), *with_peer(other)),
        (*with_peer(above), *with_peer(below)),
        (*with_peer(above_other), *with_peer(below_other)),
        (*with_peer(far), *with_peer(far_other)),
    )


def rope_tables(length):
    halfway = HEAD_DIM // 2
    indices = jnp.arange(halfway, dtype=f32)
    frequency = rope_base ** (-2.0 * indices / HEAD_DIM)
    angles = jnp.arange(length, dtype=f32)[:, None] * frequency[None, :]
    angles = jnp.concatenate([angles] * 4, axis=1)
    return (jnp.cos(angles), jnp.sin(angles))


def nt(lhs, rhs):
    return lax.dot_general(lhs, rhs, (((1,), (1,)), ((), ())), preferred_element_type=f32)


def tn(lhs, rhs):
    return lax.dot_general(lhs, rhs, (((0,), (0,)), ((), ())), preferred_element_type=f32)


def nn(lhs, rhs):
    return jnp.dot(lhs, rhs, preferred_element_type=f32)


def chip_of(at, dx, dy):
    x_at = at[0] if dx == 0 else 1 - at[0]
    return x_at * 4 + lax.rem(at[1] + dy, 4)


def qkv_block(piece, j):
    return piece[j * TILE : (j + 1) * TILE, :]


def out_block(piece, j):
    return piece[Q_ROWS + j * HEAD_DIM : Q_ROWS + (j + 1) * HEAD_DIM, :]


def inverse_rms(rows):
    return lax.rsqrt(jnp.mean(rows * rows, axis=-1, keepdims=True) + rms_eps)


def chips_of(at, keys):
    return [chip_of(at, dx, dy) for pair in keys for dx, dy in pair]


def relative_columns(at, normed, keys, rel):
    core = at[2]
    for n, chip in enumerate(chips_of(at, keys)):
        for half, place in ((0, core), (1, 1 - core)):
            cols = pl.ds(pl.multiple_of((chip * 2 + place) * TILE, TILE), TILE)
            rel[:, (2 * n + half) * TILE : (2 * n + half + 1) * TILE] = normed[:, cols]


def project_rows(rel, pieces, acc_init, acc):
    for j in range(3):
        rows = [qkv_block(piece, j) for piece in pieces]
        cols = slice(j * BLOCK, (j + 1) * BLOCK)
        total = nn(rel, jnp.concatenate(rows, axis=0))
        if acc_init is not None:
            total = total + acc_init[:, cols]
        acc[:, cols] = total


def project_heads(at, upstream, pieces, keys, attn_grad):
    core = at[2]
    heads = None
    for j in range(4):
        rows = [out_block(piece, j) for piece in pieces]
        part = nt(upstream[:, j * BLOCK : (j + 1) * BLOCK], jnp.concatenate(rows, axis=0))
        heads = part if heads is None else heads + part
    for n, chip in enumerate(chips_of(at, keys)):
        block = heads[:, n * TILE : (n + 1) * TILE]
        block = jnp.where(core == 0, block, pltpu.roll(block, HEAD_DIM, 1))
        attn_grad[:, pl.ds(pl.multiple_of(chip * TILE, TILE), TILE)] = block.astype(bf16)


def first_body(
    at, x_all, g_all, gain, *refs
):
    pieces, (acc, attn_grad, rest, x, g, normed, rel, sems) = (refs[:8], refs[8:])
    copies = [
        pltpu.make_async_copy(x_all.at[0, at[3]], x, sems.at[0]),
        pltpu.make_async_copy(g_all.at[0, at[3]], g, sems.at[1]),
    ]
    for copy in copies:
        copy.start()
    copies[0].wait()

    def norm_rows(i, carry):
        rows = pl.ds(pl.multiple_of(i * 32, 32), 32)
        wide = x[rows, :].astype(f32)
        normed[rows, :] = (wide * inverse_rms(wide) * gain[...]).astype(bf16)
        return carry

    lax.fori_loop(0, SEQ // 32, norm_rows, 0)
    relative_columns(at, normed, GROUPS[:2], rel)
    relative_columns(at, normed, GROUPS[2:], rest)
    project_rows(rel[...], pieces, None, acc)
    copies[1].wait()
    project_heads(at, g, pieces, GROUPS[:2], attn_grad)


def first_stage(at, layer_inputs, out_grads, gain, groups):
    pieces = [array for pair in groups for array in pair]
    return pl.pallas_call(
        first_body,
        in_specs=[SMEM, HBM, HBM] + [VMEM] * (1 + 8),
        out_specs=[VMEM] * 3,
        out_shape=[
            jax.ShapeDtypeStruct((SEQ, WIDTH), f32),
            jax.ShapeDtypeStruct((SEQ, QW), bf16),
            jax.ShapeDtypeStruct((SEQ, QW), bf16),
        ],
        scratch_shapes=[
            pltpu.VMEM((SEQ, D), bf16),
            pltpu.VMEM((SEQ, D), bf16),
            pltpu.VMEM((SEQ, D), bf16),
            pltpu.VMEM((SEQ, QW), bf16),
            pltpu.SemaphoreType.DMA((2,)),
        ],
        compiler_params=limit(24),
        name="first_stage",
    )(at, layer_inputs, out_grads, gain, *pieces)


def more_body(at, g_all, acc_in, attn_in, rest, *refs):
    pieces, (acc, attn_grad, g, sems) = (refs[:4], refs[4:])
    copy = pltpu.make_async_copy(g_all.at[0, at[3]], g, sems.at[0])
    copy.start()
    attn_grad[...] = attn_in[...]
    project_rows(rest[:, : 4 * TILE], pieces, acc_in, acc)
    copy.wait()
    project_heads(at, g, pieces, GROUPS[2:3], attn_grad)


def more_stage(at, out_grads, acc, attn_grad, rest, group):
    return pl.pallas_call(
        more_body,
        in_specs=[SMEM, HBM] + [VMEM] * 7,
        out_specs=[VMEM] * 2,
        out_shape=[jax.ShapeDtypeStruct((SEQ, WIDTH), f32), jax.ShapeDtypeStruct((SEQ, QW), bf16)],
        scratch_shapes=[pltpu.VMEM((SEQ, D), bf16), pltpu.SemaphoreType.DMA((1,))],
        compiler_params=limit(20),
        name="more_stage",
    )(at, out_grads, acc, attn_grad, rest, *group)


def whole_spec(shape):
    return pl.BlockSpec(shape, lambda i, at: (0,) * len(shape))


def first_half_lanes(rows):
    lanes = lax.broadcasted_iota(jnp.int32, (rows, TILE), 1)
    return lax.rem(lanes, HEAD_DIM) < HEAD_DIM // 2


def rope(u, cosine, sine):
    turned = jnp.where(
        first_half_lanes(u.shape[0]), -pltpu.roll(u, TILE - 32, 1), pltpu.roll(u, 32, 1)
    )
    return u * cosine + turned * sine


def unrope(u, cosine, sine):
    v = u * sine
    turned = jnp.where(
        first_half_lanes(u.shape[0]), -pltpu.roll(v, TILE - 32, 1), pltpu.roll(v, 32, 1)
    )
    return u * cosine - turned


def lower_lanes(rows):
    return lax.broadcasted_iota(jnp.int32, (rows, TILE), 1) < HEAD_DIM


def key_half(block, odd):
    wide = block.astype(f32)
    if odd:
        wide = pltpu.roll(wide, HEAD_DIM, 1)
    return jnp.where(lower_lanes(block.shape[0]), wide, 0.0)


def lane_block(block):
    return pl.ds(pl.multiple_of(block * TILE, TILE), TILE)


def stacked_heads(source, tile_rows, group):
    parts = []
    for pair in range(2):
        block = source[tile_rows, lane_block(2 * group + pair)]
        parts += [block, pltpu.roll(block.astype(f32), HEAD_DIM, 1).astype(bf16)]
    return jnp.concatenate(parts, axis=0)


def attention_tile(qkv, attn_grad, tile, both, odd, grad_q, grad_k, grad_v, fresh):
    count = (tile + 1) * TILE
    tile_rows = slice(tile * TILE, count)
    group = 2 * both + odd
    keys = (key_half(qkv[:count, lane_block(8 + both)], odd) * 0.125).astype(bf16)
    values = key_half(qkv[:count, lane_block(10 + both)], odd).astype(bf16)
    queries = stacked_heads(qkv, tile_rows, group)
    grads = stacked_heads(attn_grad, tile_rows, group)
    weights = jnp.exp(nt(keys, queries))
    key_ids = lax.broadcasted_iota(jnp.int32, (TILE, 4 * TILE), 0)
    query_ids = lax.rem(lax.broadcasted_iota(jnp.int32, (TILE, 4 * TILE), 1), TILE)
    last = jnp.where(key_ids <= query_ids, weights[tile * TILE :], 0.0)
    weights = last if tile == 0 else jnp.concatenate([weights[: tile * TILE], last], axis=0)
    probs = weights * (1.0 / jnp.sum(weights, axis=0, keepdims=True))
    grad_probs = nt(values, grads)
    delta = jnp.sum(probs * grad_probs, axis=0, keepdims=True)
    grad_scores = (probs * (grad_probs - delta)).astype(bf16)
    value_part = nn(probs.astype(bf16), grads)
    key_part = nn(grad_scores, queries) * 0.125
    if fresh:
        grad_v[group, :count, :] = value_part
        grad_k[group, :count, :] = key_part
    else:
        grad_v[group, :count, :] += value_part
        grad_k[group, :count, :] += key_part
    turned = tn(keys, grad_scores)[:HEAD_DIM]
    for pair in range(2):
        both = jnp.concatenate(
            [turned[:, (2 * pair + i) * TILE : (2 * pair + i + 1) * TILE] for i in range(2)], axis=0
        )
        grad_q(2 * group + pair, both.T)


def finish_rows(at, rows, grad_proj, pieces, x, g, gain, grad_normed, out):
    core = at[2]
    for n, chip in enumerate(chips_of(at, GROUPS)):
        both = jnp.concatenate(
            [
                jnp.concatenate([qkv_block(piece, j) for j in range(3)], axis=1)
                for piece in pieces[2 * n : 2 * n + 2]
            ],
            axis=0,
        )
        part = nt(grad_proj[...], both)
        for half, place in ((0, core), (1, 1 - core)):
            cols = pl.ds(pl.multiple_of((chip * 2 + place) * TILE, TILE), TILE)
            grad_normed[:, cols] = part[:, half * TILE : (half + 1) * TILE]

    def norm_rows(i, carry):
        here = pl.ds(pl.multiple_of(i * 16, 16), 16)
        wide = x[here, :].astype(f32)
        inv = inverse_rms(wide)
        scaled = grad_normed[here, :] * gain[...]
        inner = jnp.mean(scaled * wide, axis=-1, keepdims=True)
        result = g[here, :].astype(f32) + inv * scaled - wide * (inv * inv * inv * inner)
        out[here, :] = result.astype(bf16)
        return carry

    lax.fori_loop(0, rows // 16, norm_rows, 0)


def join_keys(grad_k, grad_v, rows, cosine, sine, grad_proj):
    lower = lower_lanes(TILE)
    for pair in range(2):
        for first in range(rows[0], rows[1], TILE):
            here = slice(first, first + TILE)
            there = slice(first - rows[0], first - rows[0] + TILE)
            k = jnp.where(
                lower,
                grad_k[2 * pair, here, :],
                pltpu.roll(grad_k[2 * pair + 1, here, :], HEAD_DIM, 1),
            )
            v = jnp.where(
                lower,
                grad_v[2 * pair, here, :],
                pltpu.roll(grad_v[2 * pair + 1, here, :], HEAD_DIM, 1),
            )
            at_key = QW + pair * TILE
            grad_proj[there, at_key : at_key + TILE] = unrope(
                k, cosine[here, :], sine[here, :]
            ).astype(bf16)
            grad_proj[there, at_key + 2 * TILE : at_key + 3 * TILE] = v.astype(bf16)


def store_query_grads(grad_proj, there, cosine, sine):
    def store(block, value):
        grad_proj[there, lane_block(block)] = unrope(value, cosine, sine).astype(bf16)

    return store


def second_body(
    at, x_all, g_all, gain, cosine, sine, acc_in, attn_in, rest, *refs
):
    pieces, (out, qkv_first, attn_first, grad_k_first, grad_v_first) = (refs[:16], refs[16:21])
    x, g, acc, attn_grad, qkv, grad_k, grad_v, grad_proj, grad_normed, sems = refs[21:]
    slot = at[3]
    copies = [
        pltpu.make_async_copy(g_all.at[0, slot], g, sems.at[1]),
        pltpu.make_async_copy(x_all.at[0, slot, pl.ds(TILE, 2 * TILE)], x, sems.at[0]),
    ]
    for copy in copies:
        copy.start()
    attn_grad[...] = attn_in[...]
    project_rows(rest[:, 4 * TILE :], pieces[12:], acc_in, acc)
    for block in range(10):
        cols = slice(block * TILE, (block + 1) * TILE)
        qkv[:, cols] = rope(acc[:, cols], cosine[...], sine[...]).astype(bf16)
    qkv[:, 10 * TILE :] = acc[:, 10 * TILE :].astype(bf16)
    copies[0].wait()
    project_heads(at, g, pieces[12:], GROUPS[3:], attn_grad)

    def two_groups(both, carry):
        for tile in (2, 1):
            here = slice(tile * TILE, (tile + 1) * TILE)
            there = slice((tile - 1) * TILE, tile * TILE)
            store = store_query_grads(grad_proj, there, cosine[here, :], sine[here, :])
            for odd in range(2):
                attention_tile(qkv, attn_grad, tile, both, odd, store, grad_k, grad_v, tile == 2)
        return carry

    lax.fori_loop(0, 2, two_groups, 0)
    join_keys(grad_k, grad_v, (TILE, SEQ), cosine, sine, grad_proj)
    copies[1].wait()
    finish_rows(at, 2 * TILE, grad_proj, pieces, x, g.at[TILE:], gain, grad_normed, out)
    qkv_first[...] = qkv[:TILE, :]
    attn_first[...] = attn_grad[:TILE, :]
    grad_k_first[...] = grad_k[:, :TILE, :]
    grad_v_first[...] = grad_v[:, :TILE, :]


def second_stage(at, layer_inputs, out_grads, gain, tables, acc, attn_grad, rest, groups):
    pieces = [array for pair in groups for array in pair]
    return pl.pallas_call(
        second_body,
        in_specs=[SMEM, HBM, HBM] + [VMEM] * (6 + 16),
        out_specs=[VMEM] * 5,
        out_shape=[
            jax.ShapeDtypeStruct((2 * TILE, D), bf16),
            jax.ShapeDtypeStruct((TILE, WIDTH), bf16),
            jax.ShapeDtypeStruct((TILE, QW), bf16),
            jax.ShapeDtypeStruct((KV_HEADS, TILE, TILE), f32),
            jax.ShapeDtypeStruct((KV_HEADS, TILE, TILE), f32),
        ],
        scratch_shapes=[
            pltpu.VMEM((2 * TILE, D), bf16),
            pltpu.VMEM((SEQ, D), bf16),
            pltpu.VMEM((SEQ, WIDTH), f32),
            pltpu.VMEM((SEQ, QW), bf16),
            pltpu.VMEM((SEQ, WIDTH), bf16),
            pltpu.VMEM((KV_HEADS, SEQ, TILE), f32),
            pltpu.VMEM((KV_HEADS, SEQ, TILE), f32),
            pltpu.VMEM((2 * TILE, WIDTH), bf16),
            pltpu.VMEM((2 * TILE, D), f32),
            pltpu.SemaphoreType.DMA((2,)),
        ],
        compiler_params=limit(24),
        name="second_stage",
    )(at, layer_inputs, out_grads, gain, *tables, acc, attn_grad, rest, *pieces)


def third_body(
    at, x_all, g_all, gain, cosine, sine, qkv, attn_grad, grad_k_in, grad_v_in, *refs
):
    pieces, (out, x, g, grad_k, grad_v, grad_proj, grad_normed, sems) = (refs[:16], refs[16:])
    slot = at[3]
    copies = [
        pltpu.make_async_copy(x_all.at[0, slot, pl.ds(0, TILE)], x, sems.at[0]),
        pltpu.make_async_copy(g_all.at[0, slot, pl.ds(0, TILE)], g, sems.at[1]),
    ]
    for copy in copies:
        copy.start()
    grad_k[...] = grad_k_in[...]
    grad_v[...] = grad_v_in[...]
    here = slice(0, TILE)
    store = store_query_grads(grad_proj, here, cosine[here, :], sine[here, :])

    def two_groups(both, carry):
        for odd in range(2):
            attention_tile(qkv, attn_grad, 0, both, odd, store, grad_k, grad_v, False)
        return carry

    lax.fori_loop(0, 2, two_groups, 0)
    join_keys(grad_k, grad_v, (0, TILE), cosine, sine, grad_proj)
    for copy in copies:
        copy.wait()
    finish_rows(at, TILE, grad_proj, pieces, x, g, gain, grad_normed, out)


def third_stage(at, layer_inputs, out_grads, gain, tables, carried, groups):
    pieces = [array for pair in groups for array in pair]
    return pl.pallas_call(
        third_body,
        in_specs=[SMEM, HBM, HBM] + [VMEM] * (7 + 16),
        out_specs=VMEM,
        out_shape=jax.ShapeDtypeStruct((TILE, D), bf16),
        scratch_shapes=[
            pltpu.VMEM((TILE, D), bf16),
            pltpu.VMEM((TILE, D), bf16),
            pltpu.VMEM((KV_HEADS, TILE, TILE), f32),
            pltpu.VMEM((KV_HEADS, TILE, TILE), f32),
            pltpu.VMEM((TILE, WIDTH), bf16),
            pltpu.VMEM((TILE, D), f32),
            pltpu.SemaphoreType.DMA((2,)),
        ],
        compiler_params=limit(24),
        name="third_stage",
    )(at, layer_inputs, out_grads, gain, *tables, *carried, *pieces)


def weight_body(at, x_all, p_all, a_all, e_all, gain, sent, kept, x, p, a, e, inv, sems):
    step = pl.program_id(0)
    slot = at[3]
    copies = [
        pltpu.make_async_copy(whole.at[0, slot], part, sems.at[n])
        for n, (whole, part) in enumerate(((x_all, x), (p_all, p), (a_all, a), (e_all, e)))
    ]

    @pl.when(step == 0)
    def _():
        for copy in copies:
            copy.start()
        copies[0].wait()

        def norm_rows(i, carry):
            rows = pl.ds(pl.multiple_of(i * 32, 32), 32)
            inv[rows, :] = jnp.broadcast_to(inverse_rms(x[rows, :].astype(f32)), (32, TILE))
            return carry

        lax.fori_loop(0, SEQ // 32, norm_rows, 0)
        for copy in copies[1:]:
            copy.wait()

    flip = lax.rem(step, 2)
    x_at = at[0] + flip - 2 * at[0] * flip
    chip = x_at * 4 + lax.rem(at[1] + step // 2, 4)
    cols = pl.ds(pl.multiple_of(chip * 2 * TILE, 2 * TILE), 2 * TILE)
    scale = jnp.concatenate([inv[...], inv[...]], axis=1)
    normed = (x[:, cols].astype(f32) * scale * gain[:, cols]).astype(bf16)
    part = tn(normed, p[...])
    core_zero = at[2] == 0
    for j in range(3):
        where = slice(j * TILE, (j + 1) * TILE)
        top = part[:TILE, j * BLOCK : (j + 1) * BLOCK].astype(bf16)
        low = part[TILE:, j * BLOCK : (j + 1) * BLOCK].astype(bf16)
        kept[0, where, :] = jnp.where(core_zero, top, low)
        sent[0, where, :] = jnp.where(core_zero, low, top)
    heads = a[:, pl.ds(pl.multiple_of(chip * TILE, TILE), TILE)]
    part = tn(heads, e[...])
    for j in range(4):
        where = slice(Q_ROWS + j * HEAD_DIM, Q_ROWS + (j + 1) * HEAD_DIM)
        top = part[:HEAD_DIM, j * BLOCK : (j + 1) * BLOCK].astype(bf16)
        low = part[HEAD_DIM:, j * BLOCK : (j + 1) * BLOCK].astype(bf16)
        kept[0, where, :] = jnp.where(core_zero, top, low)
        sent[0, where, :] = jnp.where(core_zero, low, top)


def weight_stage(at, layer_inputs, proj_grads, attn_stash, out_grads, gain):
    block = pl.BlockSpec((1, PIECE, BLOCK), lambda i, at: (lax.rem(i, 2) * 4 + i // 2, 0, 0))
    shape = jax.ShapeDtypeStruct((8, PIECE, BLOCK), bf16)
    return pl.pallas_call(
        weight_body,
        grid_spec=pltpu.PrefetchScalarGridSpec(
            num_scalar_prefetch=1,
            grid=(8,),
            in_specs=[HBM] * 4 + [whole_spec((1, D))],
            out_specs=[block, block],
            scratch_shapes=[
                pltpu.VMEM((SEQ, D), bf16),
                pltpu.VMEM((SEQ, WIDTH), bf16),
                pltpu.VMEM((SEQ, QW), bf16),
                pltpu.VMEM((SEQ, D), bf16),
                pltpu.VMEM((SEQ, TILE), f32),
                pltpu.SemaphoreType.DMA((4,)),
            ],
        ),
        out_shape=[shape, shape],
        compiler_params=limit(56),
        name="weight_stage",
    )(at, layer_inputs, proj_grads, attn_stash, out_grads, gain)


def wide(array):
    return array.astype(f32)


def prepare_body(kept, received, up, down, k, r, sems):
    copies = []
    for n in range(2):
        far = (4 * n + 2, pl.ds(0, Q_ROWS))
        copies.append(pltpu.make_async_copy(kept.at[far], k.at[n], sems.at[2 * n]))
        copies.append(pltpu.make_async_copy(received.at[far], r.at[n], sems.at[2 * n + 1]))
    for copy in copies:
        copy.start()
    for copy in copies:
        copy.wait()
    for n, out in enumerate((up, down)):
        out[...] = (wide(k[n]) + wide(r[n])).astype(bf16)


def prepare_stage(kept, received):
    shape = jax.ShapeDtypeStruct((Q_ROWS, BLOCK), bf16)
    return pl.pallas_call(
        prepare_body,
        in_specs=[HBM] * 2,
        out_specs=[VMEM] * 2,
        out_shape=[shape, shape],
        scratch_shapes=[
            pltpu.VMEM((2, Q_ROWS, BLOCK), bf16),
            pltpu.VMEM((2, Q_ROWS, BLOCK), bf16),
            pltpu.SemaphoreType.DMA((4,)),
        ],
        compiler_params=limit(10),
        name="prepare",
    )(kept, received)


def final_body(mine, last, qkv):
    total = mine[...] + last[...].astype(f32)
    for j in range(3):
        qkv[0, :, j * BLOCK : (j + 1) * BLOCK] = total[j * TILE : (j + 1) * TILE]


def final_sum(mine, last):
    return pl.pallas_call(
        final_body,
        in_specs=[VMEM] * 2,
        out_specs=VMEM,
        out_shape=jax.ShapeDtypeStruct((1, TILE, WIDTH), f32),
        compiler_params=limit(6),
        name="final_sum",
    )(mine, last)


def out_body(mine, far, above, below, out):
    total = mine[...] + wide(far[...]) + wide(above[...]) + wide(below[...])
    for j in range(4):
        out[0, :, j * BLOCK : (j + 1) * BLOCK] = total[j * HEAD_DIM : (j + 1) * HEAD_DIM]


def out_total(*arrays):
    return pl.pallas_call(
        out_body,
        in_specs=[VMEM] * 4,
        out_specs=VMEM,
        out_shape=jax.ShapeDtypeStruct((1, HEAD_DIM, D), f32),
        compiler_params=limit(6),
        name="out_total",
    )(*arrays)


def scattered(sent, kept):
    received = passed_along(sent, "core", 1)
    across = (wide(kept[4:, Q_ROWS:]) + wide(received[4:, Q_ROWS:])).astype(bf16)
    across = passed_along(across, "x_hi", 1)
    up, down = prepare_stage(kept, received)
    up = wide(from_below(up))
    down = wide(from_above(down))

    def qkv_sum(dx, dy):
        at = 4 * dx + dy
        return wide(kept[at, :Q_ROWS]) + wide(received[at, :Q_ROWS])

    def out_sum(dy):
        return wide(kept[dy, Q_ROWS:]) + wide(received[dy, Q_ROWS:]) + wide(across[dy])

    above = jnp.concatenate([qkv_sum(0, 1) + up, qkv_sum(1, 1)])
    below = jnp.concatenate([qkv_sum(0, 3), qkv_sum(1, 3) + down])
    above = wide(from_below(above.astype(bf16)))
    below = wide(from_above(below.astype(bf16)))
    out_far = passed_along(out_sum(2).astype(bf16), "y", 2)
    out_above = from_below(out_sum(1).astype(bf16))
    out_below = from_above(out_sum(3).astype(bf16))
    kept_rows = qkv_sum(0, 0) + above[:Q_ROWS] + below[:Q_ROWS]
    sent_rows = qkv_sum(1, 0) + above[Q_ROWS:] + below[Q_ROWS:]
    last = passed_along(sent_rows.astype(bf16), "x_hi", 1)
    return (final_sum(kept_rows, last), out_total(out_sum(0), out_far, out_above, out_below))


def local_step(
    layer_inputs, out_grads, attn_stash, proj_grads, w_qkv, w_out, norm_gain, b_sched, w_sched
):
    tables = rope_tables(SEQ)
    place = [lax.axis_index(name) for name in FSDP]
    at_b = jnp.stack([*place, b_sched[0]]).astype(jnp.int32)
    at_w = jnp.stack([*place, w_sched[0]]).astype(jnp.int32)
    groups = gathered_groups(packed_shard(w_qkv, w_out))
    sent, kept = weight_stage(at_w, layer_inputs, proj_grads, attn_stash, out_grads, norm_gain)
    acc, attn_grad, rest = first_stage(at_b, layer_inputs, out_grads, norm_gain, groups[:2])
    acc, attn_grad = more_stage(at_b, out_grads, acc, attn_grad, rest, groups[2])
    grads = scattered(sent, kept)
    second, *carried = second_stage(
        at_b, layer_inputs, out_grads, norm_gain, tables, acc, attn_grad, rest, groups
    )
    second = passed_along(second, SECTION, -1)
    first = third_stage(at_b, layer_inputs, out_grads, norm_gain, tables, carried, groups)
    first = passed_along(first, SECTION, -1)
    sent_back = jnp.concatenate([first, second], axis=0)
    return (sent_back[None], *grads)


def solution(mesh):
    finer = Mesh(mesh.devices.reshape(mesh.shape["section"] // 2, 2, 2, 4, 2), SECTION + FSDP)
    return jax.shard_map(
        local_step,
        mesh=finer,
        in_specs=(
            P(SECTION, None, FSDP, None),
            P(SECTION, None, FSDP, None),
            P(SECTION, None, FSDP, None),
            P(SECTION, None, FSDP, None),
            P(SECTION, FSDP, None),
            P(SECTION, FSDP, None),
            P(SECTION, None),
            P(SECTION),
            P(SECTION),
        ),
        out_specs=(P(SECTION, FSDP, None), P(SECTION, FSDP, None), P(SECTION, FSDP, None)),
        check_vma=False,
    )
```

profile of v0, /device:TPU:1, one launch (start us, length us, event | category | flops | bytes accessed | tf_op | source)
XLA Modules:
  0.0 162.9 jit_solution(13027363851224456693)
XLA Ops:
  1.9 13.4 %weight_stage.1 = (bf16[8,640,512]{2,1,0:T(8,128)(2,1)}, bf16[8,640,512]{2,1,0:T(8,128)(2,1)}) custom-call(s32[4]{0:T(128)} %get-tuple-element.31.at, bf16[1,2,384,2048]{3,2,1,0:T(8,128)(2,1)} %x_all.7, bf16[1,2,384,1536]{3,2,1,0:T(8,128)(2,1)} %p_all.1, bf16[1,2,384,1024]{3,2,1,0:T(8,128)(2,1)} %a_all.1, bf16[1,2,384,2048]{3,2,1,0:T(8,128)(2,1)} %e_all.1, ...), custom_call_target="tpu_custom_call" | custom-call | tf_op jit(solution)/shard_map/weight_stage/pallas_call | solution.py:543
  15.2 3.3 %collective-permute-start.17 = (bf16[8,640,512]{2,1,0:T(8,128)(2,1)}, bf16[8,640,512]{2,1,0:T(8,128)(2,1)S(1)}, u32[]{:S(2)}, u32[]{:S(2)}) collective-permute-start(bf16[8,640,512]{2,1,0:T(8,128)(2,1)} %get-tuple-element.28), channel_id=1, source_target_pairs={{0,1},{1,0},{2,3},{3,2},{4,5},{5,4},{6,7},{7,6},{8,9},{9,8},{10,11... | collective-permute-start | bytes 15728648 | tf_op jit(solution)/shard_map/ppermute | solution.py:38
  20.0 2.7 %collective-permute-start.3 = (bf16[640,512]{1,0:T(8,128)(2,1)S(1)}, bf16[640,512]{1,0:T(8,128)(2,1)S(1)}, u32[]{:S(2)}, u32[]{:S(2)}) collective-permute-start(bf16[640,512]{1,0:T(8,128)(2,1)S(1)} %pack.1.refs_0_), channel_id=1, source_target_pairs={{0,6},{2,0},{4,2},{6,4},{1,7},{3,1},{5,3},{7,5},{8,14},{10,8},{12,... | collective-permute-start | bytes 1966088 | tf_op jit(solution)/shard_map/ppermute | solution.py:38
  22.8 13.7 %collective-permute-done.1.refs_2_ = bf16[640,512]{1,0:T(8,128)(2,1)S(1)} collective-permute-done((bf16[640,512]{1,0:T(8,128)(2,1)S(1)}, bf16[640,512]{1,0:T(8,128)(2,1)S(1)}, u32[]{:S(2)}, u32[]{:S(2)}) %collective-permute-start.1) | collective-permute-done | bytes 655392 | tf_op jit(solution)/shard_map/ppermute | solution.py:38
  37.7 2.1 %collective-permute-done.5.refs_6_ = bf16[640,512]{1,0:T(8,128)(2,1)S(1)} collective-permute-done((bf16[640,512]{1,0:T(8,128)(2,1)S(1)}, bf16[640,512]{1,0:T(8,128)(2,1)S(1)}, u32[]{:S(2)}, u32[]{:S(2)}) %collective-permute-start.5) | collective-permute-done | bytes 655392 | tf_op jit(solution)/shard_map/ppermute | solution.py:38
  39.8 1.3 collective-permute-start.7
  41.1 12.7 %collective-permute-done.9.refs_2_.refs_10_ = bf16[640,512]{1,0:T(8,128)(2,1)S(1)} collective-permute-done((bf16[640,512]{1,0:T(8,128)(2,1)S(1)}, bf16[640,512]{1,0:T(8,128)(2,1)S(1)}, u32[]{:S(2)}, u32[]{:S(2)}) %collective-permute-start.9) | collective-permute-done | bytes 655392 | tf_op jit(solution)/shard_map/ppermute | solution.py:38
  53.8 1.5 collective-permute-start.13
  55.3 2.5 %copy-done.2 = bf16[8,640,512]{2,1,0:T(8,128)(2,1)S(1)} copy-done((bf16[8,640,512]{2,1,0:T(8,128)(2,1)S(1)}, bf16[8,640,512]{2,1,0:T(8,128)(2,1)}, u32[]{:S(2)}) %copy-start.2) | copy-done | bytes 5242904
  58.9 2.6 %collective-permute-start.20 = (bf16[384,512]{1,0:T(8,128)(2,1)S(1)}, bf16[384,512]{1,0:T(8,128)(2,1)S(1)}, u32[]{:S(2)}, u32[]{:S(2)}) collective-permute-start(bf16[384,512]{1,0:T(8,128)(2,1)S(1)} %get-tuple-element.30), channel_id=1, source_target_pairs={{0,6},{2,0},{4,2},{6,4},{1,7},{3,1},{5,3},{7,5},{8,14},{10,8},{12,... | collective-permute-start | bytes 1179656 | tf_op jit(solution)/shard_map/ppermute | solution.py:38
  61.9 2.6 %collective-permute-start.6 = (bf16[640,512]{1,0:T(8,128)(2,1)S(1)}, bf16[640,512]{1,0:T(8,128)(2,1)S(1)}, u32[]{:S(2)}, u32[]{:S(2)}) collective-permute-start(bf16[640,512]{1,0:T(8,128)(2,1)S(1)} %collective-permute-done.5.refs_6_), channel_id=1, source_target_pairs={{0,1},{1,0},{2,3},{3,2},{4,5},{5,4},{6,7},{7,6},{8,9},{9,8},{10,11... | collective-permute-start | bytes 1966088 | tf_op jit(solution)/shard_map/ppermute | solution.py:38
  64.5 4.7 %collective-permute-done.11.refs_12_ = bf16[640,512]{1,0:T(8,128)(2,1)S(1)} collective-permute-done((bf16[640,512]{1,0:T(8,128)(2,1)S(1)}, bf16[640,512]{1,0:T(8,128)(2,1)S(1)}, u32[]{:S(2)}, u32[]{:S(2)}) %collective-permute-start.11) | collective-permute-done | bytes 655392 | tf_op jit(solution)/shard_map/ppermute | solution.py:38
  69.2 3.6 %collective-permute-start.10 = (bf16[640,512]{1,0:T(8,128)(2,1)S(1)}, bf16[640,512]{1,0:T(8,128)(2,1)S(1)}, u32[]{:S(2)}, u32[]{:S(2)}) collective-permute-start(bf16[640,512]{1,0:T(8,128)(2,1)S(1)} %collective-permute-done.9.refs_2_.refs_10_), channel_id=1, source_target_pairs={{0,1},{1,0},{2,3},{3,2},{4,5},{5,4},{6,7},{7,6},{8,9},{9,8},{10,11... | collective-permute-start | bytes 1966088 | tf_op jit(solution)/shard_map/ppermute | solution.py:38
  74.3 4.1 %collective-permute-done.18 = bf16[384,512]{1,0:T(8,128)(2,1)S(1)} collective-permute-done((bf16[384,512]{1,0:T(8,128)(2,1)S(1)}, bf16[384,512]{1,0:T(8,128)(2,1)S(1)}, u32[]{:S(2)}, u32[]{:S(2)}) %collective-permute-start.18) | collective-permute-done | bytes 393248 | tf_op jit(solution)/shard_map/ppermute | solution.py:38
  78.4 2.2 %collective-permute-start.12 = (bf16[640,512]{1,0:T(8,128)(2,1)S(1)}, bf16[640,512]{1,0:T(8,128)(2,1)S(1)}, u32[]{:S(2)}, u32[]{:S(2)}) collective-permute-start(bf16[640,512]{1,0:T(8,128)(2,1)S(1)} %collective-permute-done.11.refs_12_), channel_id=1, source_target_pairs={{0,1},{1,0},{2,3},{3,2},{4,5},{5,4},{6,7},{7,6},{8,9},{9,8},{10,11... | collective-permute-start | bytes 1966088 | tf_op jit(solution)/shard_map/ppermute | solution.py:38
  82.9 1.7 %collective-permute-start.23 = (bf16[4,256,512]{2,1,0:T(8,128)(2,1)S(1)}, bf16[4,256,512]{2,1,0:T(8,128)(2,1)}, u32[]{:S(2)}, u32[]{:S(2)}) collective-permute-start(bf16[4,256,512]{2,1,0:T(8,128)(2,1)S(1)} %add_convert_fusion), channel_id=1, source_target_pairs={{0,8},{8,0},{1,9},{9,1},{2,10},{10,2},{3,11},{11,3},{4,12},{12,4},... | collective-permute-start | bytes 3145736 | tf_op jit(solution)/shard_map/ppermute | solution.py:38
  84.6 1.5 collective-permute-start.19
  87.7 5.2 %first_stage.1 = (f32[384,1536]{1,0:T(8,128)S(1)}, bf16[384,1024]{1,0:T(8,128)(2,1)S(1)}, bf16[384,1024]{1,0:T(8,128)(2,1)S(1)}) custom-call(s32[4]{0:T(128)S(1)} %pad_add_fusion.at, bf16[1,2,384,2048]{3,2,1,0:T(8,128)(2,1)S(1)} %copy-done.1, bf16[1,2,384,2048]{3,2,1,0:T(8,128)(2,1)S(1)} %copy-done, f32[1,2048]{1,0:T(1,128)S(1)} %copy-done.24, ...), custom_call_target="tpu_custom_call" | custom-call | tf_op jit(solution)/shard_map/first_stage/pallas_call | solution.py:193
  92.9 3.0 %more_stage.1 = (f32[384,1536]{1,0:T(8,128)S(1)}, bf16[384,1024]{1,0:T(8,128)(2,1)S(1)}) custom-call(s32[4]{0:T(128)S(1)} %pad_add_fusion.at, bf16[1,2,384,2048]{3,2,1,0:T(8,128)(2,1)S(1)} %copy-done, f32[384,1536]{1,0:T(8,128)S(1)} %get-tuple-element.17.acc_in, bf16[384,1024]{1,0:T(8,128)(2,1)S(1)} %get-tuple-element.18.attn_in, ...), custom_call_target="tpu_custom_call" | custom-call | tf_op jit(solution)/shard_map/more_stage/pallas_call | solution.py:225
  95.9 1.4 copy-done.20
  100.6 1.7 %copy-done.21 = f32[384,1536]{1,0:T(8,128)S(1)} copy-done((f32[384,1536]{1,0:T(8,128)S(1)}, f32[384,1536]{1,0:T(8,128)}, u32[]{:S(2)}) %copy-start.21) | copy-done | bytes 2359320
  102.3 13.0 %second_stage.1 = (bf16[256,2048]{1,0:T(8,128)(2,1)S(1)}, bf16[128,1536]{1,0:T(8,128)(2,1)S(1)}, bf16[128,1024]{1,0:T(8,128)(2,1)S(1)}, f32[4,128,128]{2,1,0:T(8,128)S(1)}, f32[4,128,128]{2,1,0:T(8,128)S(1)}) custom-call(s32[4]{0:T(128)S(1)} %pad_add_fusion.at, bf16[1,2,384,2048]{3,2,1,0:T(8,128)(2,1)S(1)} %copy-done.1, ...), custom_call_target="tpu_custom_call" | custom-call | tf_op jit(solution)/shard_map/second_stage/pallas_call | solution.py:416
  115.3 5.9 %collective-permute-start.16 = (bf16[256,2048]{1,0:T(8,128)(2,1)S(1)}, bf16[256,2048]{1,0:T(8,128)(2,1)S(1)}, u32[]{:S(2)}, u32[]{:S(2)}) collective-permute-start(bf16[256,2048]{1,0:T(8,128)(2,1)S(1)} %get-tuple-element.26), channel_id=1, source_target_pairs={{0,240},{16,0},{32,16},{48,32},{64,48},{80,64},{96,80},{112,96},{1... | collective-permute-start | bytes 3145736 | tf_op jit(solution)/shard_map/ppermute | solution.py:38
  122.3 6.2 %third_stage.1 = bf16[128,2048]{1,0:T(8,128)(2,1)S(1)} custom-call(s32[4]{0:T(128)S(1)} %pad_add_fusion.at, bf16[1,2,384,2048]{3,2,1,0:T(8,128)(2,1)S(1)} %copy-done.1, bf16[1,2,384,2048]{3,2,1,0:T(8,128)(2,1)S(1)} %copy-done, f32[1,2048]{1,0:T(1,128)S(1)} %copy-done.24, f32[384,128]{1,0:T(8,128)S(1)} %get-tuple-element.44.cosine, ...), custom_call_target="tpu_custom_call" | custom-call | tf_op jit(solution)/shard_map/third_stage/pallas_call | solution.py:474
  129.7 1.3 convert_element_type.153
  133.0 1.4 collective-permute-start.22
  134.4 1.6 fusion.7
  136.0 1.4 collective-permute-start.24
  137.3 1.8 %collective-permute-start.25 = (bf16[256,512]{1,0:T(8,128)(2,1)S(1)}, bf16[256,512]{1,0:T(8,128)(2,1)S(1)}, u32[]{:S(2)}, u32[]{:S(2)}) collective-permute-start(bf16[256,512]{1,0:T(8,128)(2,1)S(1)} %get-tuple-element.36), channel_id=1, source_target_pairs={{0,2},{2,4},{4,6},{6,0},{1,3},{3,5},{5,7},{7,1},{8,10},{10,12},{12... | collective-permute-start | bytes 786440 | tf_op jit(solution)/shard_map/ppermute | solution.py:38
  139.1 14.5 %collective-permute-done.15 = bf16[128,2048]{1,0:T(8,128)(2,1)S(1)} collective-permute-done((bf16[128,2048]{1,0:T(8,128)(2,1)S(1)}, bf16[128,2048]{1,0:T(8,128)(2,1)S(1)}, u32[]{:S(2)}, u32[]{:S(2)}) %collective-permute-start.15) | collective-permute-done | bytes 524320 | tf_op jit(solution)/shard_map/ppermute | solution.py:38
  153.6 2.4 %collective-permute-start.26 = (bf16[256,512]{1,0:T(8,128)(2,1)S(1)}, bf16[256,512]{1,0:T(8,128)(2,1)S(1)}, u32[]{:S(2)}, u32[]{:S(2)}) collective-permute-start(bf16[256,512]{1,0:T(8,128)(2,1)S(1)} %get-tuple-element.35), channel_id=1, source_target_pairs={{0,6},{2,0},{4,2},{6,4},{1,7},{3,1},{5,3},{7,5},{8,14},{10,8},{12,... | collective-permute-start | bytes 786440 | tf_op jit(solution)/shard_map/ppermute | solution.py:38
  157.3 2.6 %collective-permute-done.26.below = bf16[256,512]{1,0:T(8,128)(2,1)S(1)} collective-permute-done((bf16[256,512]{1,0:T(8,128)(2,1)S(1)}, bf16[256,512]{1,0:T(8,128)(2,1)S(1)}, u32[]{:S(2)}, u32[]{:S(2)}) %collective-permute-start.26) | collective-permute-done | bytes 262176 | tf_op jit(solution)/shard_map/ppermute | solution.py:38
  (96 shorter events, 21.2 us)
Async XLA Ops:
  15.2 38.6 %collective-permute-start.17 = (bf16[8,640,512]{2,1,0:T(8,128)(2,1)}, bf16[8,640,512]{2,1,0:T(8,128)(2,1)S(1)}, u32[]{:S(2)}, u32[]{:S(2)}) collective-permute-start(bf16[8,640,512]{2,1,0:T(8,128)(2,1)} %get-tuple-element.28), channel_id=1, source_target_pairs={{0,1},{1,0},{2,3},{3,2},{4,5},{5,4},{6,7},{7,6},{8,9},{9,8},{10,11... | collective-permute-start | bytes 15728648 | tf_op jit(solution)/shard_map/ppermute | solution.py:38
  18.6 17.9 %collective-permute-start.1 = (bf16[640,512]{1,0:T(8,128)(2,1)S(1)}, bf16[640,512]{1,0:T(8,128)(2,1)S(1)}, u32[]{:S(2)}, u32[]{:S(2)}) collective-permute-start(bf16[640,512]{1,0:T(8,128)(2,1)S(1)} %pack.1.refs_0_), channel_id=1, source_target_pairs={{0,8},{8,0},{1,9},{9,1},{2,10},{10,2},{3,11},{11,3},{4,12},{12,4},... | collective-permute-start | bytes 1966088 | tf_op jit(solution)/shard_map/ppermute | solution.py:38
  19.7 16.7 %collective-permute-start = (bf16[640,512]{1,0:T(8,128)(2,1)S(1)}, bf16[640,512]{1,0:T(8,128)(2,1)S(1)}, u32[]{:S(2)}, u32[]{:S(2)}) collective-permute-start(bf16[640,512]{1,0:T(8,128)(2,1)S(1)} %pack.1.refs_0_), channel_id=1, source_target_pairs={{0,1},{1,0},{2,3},{3,2},{4,5},{5,4},{6,7},{7,6},{8,9},{9,8},{10,11... | collective-permute-start | bytes 1966088 | tf_op jit(solution)/shard_map/ppermute | solution.py:38
  20.0 17.4 %collective-permute-start.3 = (bf16[640,512]{1,0:T(8,128)(2,1)S(1)}, bf16[640,512]{1,0:T(8,128)(2,1)S(1)}, u32[]{:S(2)}, u32[]{:S(2)}) collective-permute-start(bf16[640,512]{1,0:T(8,128)(2,1)S(1)} %pack.1.refs_0_), channel_id=1, source_target_pairs={{0,6},{2,0},{4,2},{6,4},{1,7},{3,1},{5,3},{7,5},{8,14},{10,8},{12,... | collective-permute-start | bytes 1966088 | tf_op jit(solution)/shard_map/ppermute | solution.py:38
  22.7 17.0 %collective-permute-start.5 = (bf16[640,512]{1,0:T(8,128)(2,1)S(1)}, bf16[640,512]{1,0:T(8,128)(2,1)S(1)}, u32[]{:S(2)}, u32[]{:S(2)}) collective-permute-start(bf16[640,512]{1,0:T(8,128)(2,1)S(1)} %pack.1.refs_0_), channel_id=1, source_target_pairs={{0,2},{2,4},{4,6},{6,0},{1,3},{3,5},{5,7},{7,1},{8,10},{10,12},{12... | collective-permute-start | bytes 1966088 | tf_op jit(solution)/shard_map/ppermute | solution.py:38
  36.4 17.4 %collective-permute-start.9 = (bf16[640,512]{1,0:T(8,128)(2,1)S(1)}, bf16[640,512]{1,0:T(8,128)(2,1)S(1)}, u32[]{:S(2)}, u32[]{:S(2)}) collective-permute-start(bf16[640,512]{1,0:T(8,128)(2,1)S(1)} %collective-permute-done.1.refs_2_), channel_id=1, source_target_pairs={{0,2},{2,4},{4,6},{6,0},{1,3},{3,5},{5,7},{7,1},{8,10},{10,12},{12... | collective-permute-start | bytes 1966088 | tf_op jit(solution)/shard_map/ppermute | solution.py:38
  36.4 51.2 %copy-start.4 = (bf16[640,512]{1,0:T(8,128)(2,1)}, bf16[640,512]{1,0:T(8,128)(2,1)S(1)}, u32[]{:S(2)}) copy-start(bf16[640,512]{1,0:T(8,128)(2,1)S(1)} %collective-permute-done.refs_1_) | copy-start | bytes 1966084
  36.4 22.4 %collective-permute-start.2 = (bf16[640,512]{1,0:T(8,128)(2,1)S(1)}, bf16[640,512]{1,0:T(8,128)(2,1)S(1)}, u32[]{:S(2)}, u32[]{:S(2)}) collective-permute-start(bf16[640,512]{1,0:T(8,128)(2,1)S(1)} %collective-permute-done.1.refs_2_), channel_id=1, source_target_pairs={{0,1},{1,0},{2,3},{3,2},{4,5},{5,4},{6,7},{7,6},{8,9},{9,8},{10,11... | collective-permute-start | bytes 1966088 | tf_op jit(solution)/shard_map/ppermute | solution.py:38
  37.4 50.2 %copy-start.6 = (bf16[640,512]{1,0:T(8,128)(2,1)}, bf16[640,512]{1,0:T(8,128)(2,1)S(1)}, u32[]{:S(2)}) copy-start(bf16[640,512]{1,0:T(8,128)(2,1)S(1)} %collective-permute-done.3.refs_4_) | copy-start | bytes 1966084
  37.4 21.5 %collective-permute-start.4 = (bf16[640,512]{1,0:T(8,128)(2,1)S(1)}, bf16[640,512]{1,0:T(8,128)(2,1)S(1)}, u32[]{:S(2)}, u32[]{:S(2)}) collective-permute-start(bf16[640,512]{1,0:T(8,128)(2,1)S(1)} %collective-permute-done.3.refs_4_), channel_id=1, source_target_pairs={{0,1},{1,0},{2,3},{3,2},{4,5},{5,4},{6,7},{7,6},{8,9},{9,8},{10,11... | collective-permute-start | bytes 1966088 | tf_op jit(solution)/shard_map/ppermute | solution.py:38
  39.8 47.9 %copy-start.8 = (bf16[640,512]{1,0:T(8,128)(2,1)}, bf16[640,512]{1,0:T(8,128)(2,1)S(1)}, u32[]{:S(2)}) copy-start(bf16[640,512]{1,0:T(8,128)(2,1)S(1)} %collective-permute-done.5.refs_6_) | copy-start | bytes 1966084
  39.8 22.1 %collective-permute-start.7 = (bf16[640,512]{1,0:T(8,128)(2,1)S(1)}, bf16[640,512]{1,0:T(8,128)(2,1)S(1)}, u32[]{:S(2)}, u32[]{:S(2)}) collective-permute-start(bf16[640,512]{1,0:T(8,128)(2,1)S(1)} %collective-permute-done.1.refs_2_), channel_id=1, source_target_pairs={{0,6},{2,0},{4,2},{6,4},{1,7},{3,1},{5,3},{7,5},{8,14},{10,8},{12,... | collective-permute-start | bytes 1966088 | tf_op jit(solution)/shard_map/ppermute | solution.py:38
  53.8 39.1 %copy-start.10 = (bf16[640,512]{1,0:T(8,128)(2,1)}, bf16[640,512]{1,0:T(8,128)(2,1)S(1)}, u32[]{:S(2)}) copy-start(bf16[640,512]{1,0:T(8,128)(2,1)S(1)} %collective-permute-done.9.refs_2_.refs_10_) | copy-start | bytes 1966084
  53.8 15.4 %collective-permute-start.11 = (bf16[640,512]{1,0:T(8,128)(2,1)S(1)}, bf16[640,512]{1,0:T(8,128)(2,1)S(1)}, u32[]{:S(2)}, u32[]{:S(2)}) collective-permute-start(bf16[640,512]{1,0:T(8,128)(2,1)S(1)} %collective-permute-done.3.refs_4_), channel_id=1, source_target_pairs={{0,6},{2,0},{4,2},{6,4},{1,7},{3,1},{5,3},{7,5},{8,14},{10,8},{12,... | collective-permute-start | bytes 1966088 | tf_op jit(solution)/shard_map/ppermute | solution.py:38
  53.8 19.0 %collective-permute-start.13 = (bf16[640,512]{1,0:T(8,128)(2,1)S(1)}, bf16[640,512]{1,0:T(8,128)(2,1)S(1)}, u32[]{:S(2)}, u32[]{:S(2)}) collective-permute-start(bf16[640,512]{1,0:T(8,128)(2,1)S(1)} %collective-permute-done.9.refs_2_.refs_10_), channel_id=1, source_target_pairs={{0,2},{2,4},{4,6},{6,0},{1,3},{3,5},{5,7},{7,1},{8,10},{10,12},{12... | collective-permute-start | bytes 1966088 | tf_op jit(solution)/shard_map/ppermute | solution.py:38
  58.8 19.6 %collective-permute-start.18 = (bf16[384,512]{1,0:T(8,128)(2,1)S(1)}, bf16[384,512]{1,0:T(8,128)(2,1)S(1)}, u32[]{:S(2)}, u32[]{:S(2)}) collective-permute-start(bf16[384,512]{1,0:T(8,128)(2,1)S(1)} %get-tuple-element.29), channel_id=1, source_target_pairs={{0,2},{2,4},{4,6},{6,0},{1,3},{3,5},{5,7},{7,1},{8,10},{10,12},{12... | collective-permute-start | bytes 1179656 | tf_op jit(solution)/shard_map/ppermute | solution.py:38
  58.9 21.7 %collective-permute-start.20 = (bf16[384,512]{1,0:T(8,128)(2,1)S(1)}, bf16[384,512]{1,0:T(8,128)(2,1)S(1)}, u32[]{:S(2)}, u32[]{:S(2)}) collective-permute-start(bf16[384,512]{1,0:T(8,128)(2,1)S(1)} %get-tuple-element.30), channel_id=1, source_target_pairs={{0,6},{2,0},{4,2},{6,4},{1,7},{3,1},{5,3},{7,5},{8,14},{10,8},{12,... | collective-permute-start | bytes 1179656 | tf_op jit(solution)/shard_map/ppermute | solution.py:38
  61.9 31.0 %copy-start.15 = (bf16[640,512]{1,0:T(8,128)(2,1)}, bf16[640,512]{1,0:T(8,128)(2,1)S(1)}, u32[]{:S(2)}) copy-start(bf16[640,512]{1,0:T(8,128)(2,1)S(1)} %collective-permute-done.7.refs_0_.refs_8_) | copy-start | bytes 1966084
  61.9 21.0 %collective-permute-start.6 = (bf16[640,512]{1,0:T(8,128)(2,1)S(1)}, bf16[640,512]{1,0:T(8,128)(2,1)S(1)}, u32[]{:S(2)}, u32[]{:S(2)}) collective-permute-start(bf16[640,512]{1,0:T(8,128)(2,1)S(1)} %collective-permute-done.5.refs_6_), channel_id=1, source_target_pairs={{0,1},{1,0},{2,3},{3,2},{4,5},{5,4},{6,7},{7,6},{8,9},{9,8},{10,11... | collective-permute-start | bytes 1966088 | tf_op jit(solution)/shard_map/ppermute | solution.py:38
  69.2 15.5 %collective-permute-start.10 = (bf16[640,512]{1,0:T(8,128)(2,1)S(1)}, bf16[640,512]{1,0:T(8,128)(2,1)S(1)}, u32[]{:S(2)}, u32[]{:S(2)}) collective-permute-start(bf16[640,512]{1,0:T(8,128)(2,1)S(1)} %collective-permute-done.9.refs_2_.refs_10_), channel_id=1, source_target_pairs={{0,1},{1,0},{2,3},{3,2},{4,5},{5,4},{6,7},{7,6},{8,9},{9,8},{10,11... | collective-permute-start | bytes 1966088 | tf_op jit(solution)/shard_map/ppermute | solution.py:38
  72.8 11.9 %collective-permute-start.8 = (bf16[640,512]{1,0:T(8,128)(2,1)S(1)}, bf16[640,512]{1,0:T(8,128)(2,1)S(1)}, u32[]{:S(2)}, u32[]{:S(2)}) collective-permute-start(bf16[640,512]{1,0:T(8,128)(2,1)S(1)} %collective-permute-done.7.refs_0_.refs_8_), channel_id=1, source_target_pairs={{0,1},{1,0},{2,3},{3,2},{4,5},{5,4},{6,7},{7,6},{8,9},{9,8},{10,11... | collective-permute-start | bytes 1966088 | tf_op jit(solution)/shard_map/ppermute | solution.py:38
  78.4 18.9 %collective-permute-start.12 = (bf16[640,512]{1,0:T(8,128)(2,1)S(1)}, bf16[640,512]{1,0:T(8,128)(2,1)S(1)}, u32[]{:S(2)}, u32[]{:S(2)}) collective-permute-start(bf16[640,512]{1,0:T(8,128)(2,1)S(1)} %collective-permute-done.11.refs_12_), channel_id=1, source_target_pairs={{0,1},{1,0},{2,3},{3,2},{4,5},{5,4},{6,7},{7,6},{8,9},{9,8},{10,11... | collective-permute-start | bytes 1966088 | tf_op jit(solution)/shard_map/ppermute | solution.py:38
  80.7 16.7 %collective-permute-start.14 = (bf16[640,512]{1,0:T(8,128)(2,1)S(1)}, bf16[640,512]{1,0:T(8,128)(2,1)S(1)}, u32[]{:S(2)}, u32[]{:S(2)}) collective-permute-start(bf16[640,512]{1,0:T(8,128)(2,1)S(1)} %collective-permute-done.13.refs_14_), channel_id=1, source_target_pairs={{0,1},{1,0},{2,3},{3,2},{4,5},{5,4},{6,7},{7,6},{8,9},{9,8},{10,11... | collective-permute-start | bytes 1966088 | tf_op jit(solution)/shard_map/ppermute | solution.py:38
  82.9 51.5 %collective-permute-start.23 = (bf16[4,256,512]{2,1,0:T(8,128)(2,1)S(1)}, bf16[4,256,512]{2,1,0:T(8,128)(2,1)}, u32[]{:S(2)}, u32[]{:S(2)}) collective-permute-start(bf16[4,256,512]{2,1,0:T(8,128)(2,1)S(1)} %add_convert_fusion), channel_id=1, source_target_pairs={{0,8},{8,0},{1,9},{9,1},{2,10},{10,2},{3,11},{11,3},{4,12},{12,4},... | collective-permute-start | bytes 3145736 | tf_op jit(solution)/shard_map/ppermute | solution.py:38
  84.6 45.1 %collective-permute-start.21 = (bf16[768,512]{1,0:T(8,128)(2,1)}, bf16[768,512]{1,0:T(8,128)(2,1)}, u32[]{:S(2)}, u32[]{:S(2)}) collective-permute-start(bf16[768,512]{1,0:T(8,128)(2,1)} %pad_maximum_fusion.1), channel_id=1, source_target_pairs={{0,6},{2,0},{4,2},{6,4},{1,7},{3,1},{5,3},{7,5},{8,14},{10,8},{12,... | collective-permute-start | bytes 2359304 | tf_op jit(solution)/shard_map/ppermute | solution.py:38
  84.6 46.4 %collective-permute-start.19 = (bf16[768,512]{1,0:T(8,128)(2,1)}, bf16[768,512]{1,0:T(8,128)(2,1)}, u32[]{:S(2)}, u32[]{:S(2)}) collective-permute-start(bf16[768,512]{1,0:T(8,128)(2,1)} %pad_maximum_fusion), channel_id=1, source_target_pairs={{0,2},{2,4},{4,6},{6,0},{1,3},{3,5},{5,7},{7,1},{8,10},{10,12},{12... | collective-permute-start | bytes 2359304 | tf_op jit(solution)/shard_map/ppermute | solution.py:38
  115.3 40.8 %collective-permute-start.16 = (bf16[256,2048]{1,0:T(8,128)(2,1)S(1)}, bf16[256,2048]{1,0:T(8,128)(2,1)S(1)}, u32[]{:S(2)}, u32[]{:S(2)}) collective-permute-start(bf16[256,2048]{1,0:T(8,128)(2,1)S(1)} %get-tuple-element.26), channel_id=1, source_target_pairs={{0,240},{16,0},{32,16},{48,32},{64,48},{80,64},{96,80},{112,96},{1... | collective-permute-start | bytes 3145736 | tf_op jit(solution)/shard_map/ppermute | solution.py:38
  128.5 25.1 %collective-permute-start.15 = (bf16[128,2048]{1,0:T(8,128)(2,1)S(1)}, bf16[128,2048]{1,0:T(8,128)(2,1)S(1)}, u32[]{:S(2)}, u32[]{:S(2)}) collective-permute-start(bf16[128,2048]{1,0:T(8,128)(2,1)S(1)} %third_stage.1), channel_id=1, source_target_pairs={{0,240},{16,0},{32,16},{48,32},{64,48},{80,64},{96,80},{112,96},{1... | collective-permute-start | bytes 1572872 | tf_op jit(solution)/shard_map/ppermute | solution.py:38
  133.0 29.0 %collective-permute-start.22 = (bf16[384,512]{1,0:T(8,128)(2,1)S(1)}, bf16[384,512]{1,0:T(8,128)(2,1)S(1)}, u32[]{:S(2)}, u32[]{:S(2)}) collective-permute-start(bf16[384,512]{1,0:T(8,128)(2,1)S(1)} %get-tuple-element.33), channel_id=1, source_target_pairs={{0,8},{8,0},{1,9},{9,1},{2,10},{10,2},{3,11},{11,3},{4,12},{12,4},... | collective-permute-start | bytes 1179656 | tf_op jit(solution)/shard_map/ppermute | solution.py:38
  136.0 21.4 %collective-permute-start.24 = (bf16[256,512]{1,0:T(8,128)(2,1)S(1)}, bf16[256,512]{1,0:T(8,128)(2,1)S(1)}, u32[]{:S(2)}, u32[]{:S(2)}) collective-permute-start(bf16[256,512]{1,0:T(8,128)(2,1)S(1)} %get-tuple-element.37), channel_id=1, source_target_pairs={{0,4},{2,6},{4,0},{6,2},{1,5},{3,7},{5,1},{7,3},{8,12},{10,14},{12... | collective-permute-start | bytes 786440 | tf_op jit(solution)/shard_map/ppermute | solution.py:38
  137.3 20.0 %collective-permute-start.25 = (bf16[256,512]{1,0:T(8,128)(2,1)S(1)}, bf16[256,512]{1,0:T(8,128)(2,1)S(1)}, u32[]{:S(2)}, u32[]{:S(2)}) collective-permute-start(bf16[256,512]{1,0:T(8,128)(2,1)S(1)} %get-tuple-element.36), channel_id=1, source_target_pairs={{0,2},{2,4},{4,6},{6,0},{1,3},{3,5},{5,7},{7,1},{8,10},{10,12},{12... | collective-permute-start | bytes 786440 | tf_op jit(solution)/shard_map/ppermute | solution.py:38
  153.6 6.4 %collective-permute-start.26 = (bf16[256,512]{1,0:T(8,128)(2,1)S(1)}, bf16[256,512]{1,0:T(8,128)(2,1)S(1)}, u32[]{:S(2)}, u32[]{:S(2)}) collective-permute-start(bf16[256,512]{1,0:T(8,128)(2,1)S(1)} %get-tuple-element.35), channel_id=1, source_target_pairs={{0,6},{2,0},{4,2},{6,4},{1,7},{3,1},{5,3},{7,5},{8,14},{10,8},{12,... | collective-permute-start | bytes 786440 | tf_op jit(solution)/shard_map/ppermute | solution.py:38
  (20 other events, 171.7 us)
where the time goes:
time: 164 us; the launch traced here: 163 us
  waiting for transfers between devices  55.5 us (34%)
  Pallas kernels  43.5 us (27%)
  starting transfers between devices  41.3 us (25%)
  other arithmetic  10.4 us (6%)
  local copies, waits for them, and re-layouts  9.95 us (6%)
  between operations  2.28 us (1%)
    ppermute x27, waiting for transfers between devices, passed_along(): lax.ppermute(array, axis, [(i, (i + by) % size) for i in range(size)])  55.5 us
    ppermute x27, starting transfers between devices, passed_along(): lax.ppermute(array, axis, [(i, (i + by) % size) for i in range(size)])  41.3 us
    pallas_call x1, Pallas kernels, weight_stage(): pl.pallas_call(weight_body, grid_spec=pltpu.PrefetchScalarGridSpec(num_sc...  13.4 us
    pallas_call x1, Pallas kernels, second_stage(): pl.pallas_call(second_body, in_specs=[SMEM, HBM, HBM] + [VMEM] * (6 + 16)...  13 us
    unnamed x50, local copies, waits for them, and re-layouts  9.95 us
    pallas_call x1, Pallas kernels, third_stage(): pl.pallas_call(third_body, in_specs=[SMEM, HBM, HBM] + [VMEM] * (7 + 16),...  6.2 us
    pallas_call x1, Pallas kernels, first_stage(): pl.pallas_call(first_body, in_specs=[SMEM, HBM, HBM] + [VMEM] * (1 + 8),...  5.18 us
  transfers between devices with their start and end apart: 27, of which 8 were waited for; matrix products, arithmetic and copies ran while one was open for 6% of the time, Pallas kernels for 18%

commit v1 on v0

--- a/solution.py
+++ b/solution.py
@@ -1,5 +1,6 @@
 import jax
 import jax.numpy as jnp
+import numpy as np
 from jax import lax
 from jax.experimental import pallas as pl
 from jax.experimental.pallas import tpu as pltpu
@@ -90,12 +91,25 @@
 
 
 def rope_tables(length):
-    halfway = HEAD_DIM // 2
-    indices = jnp.arange(halfway, dtype=f32)
-    frequency = rope_base ** (-2.0 * indices / HEAD_DIM)
-    angles = jnp.arange(length, dtype=f32)[:, None] * frequency[None, :]
-    angles = jnp.concatenate([angles] * 4, axis=1)
-    return (jnp.cos(angles), jnp.sin(angles))
+    fine = 16
+    half = HEAD_DIM // 2
+    frequency = rope_base ** (-2.0 * np.arange(half) / HEAD_DIM)
+
+    def table(function, positions):
+        return jnp.asarray(function(positions[:, None] * frequency[None, :]), f32)
+
+    steps = (np.arange(length // fine) * fine, np.arange(fine))
+    cosines = [table(np.cos, step) for step in steps]
+    sines = [table(np.sin, step) for step in steps]
+
+    def outer(first, second):
+        return first[:, None, :] * second[None, :, :]
+
+    cosine = outer(cosines[0], cosines[1]) - outer(sines[0], sines[1])
+    sine = outer(sines[0], cosines[1]) + outer(cosines[0], sines[1])
+    return tuple(
+        jnp.concatenate([part.reshape(length, half)] * 4, axis=1) for part in (cosine, sine)
+    )
 
 
 def nt(lhs, rhs):
@@ -206,7 +220,7 @@
             pltpu.VMEM((SEQ, QW), bf16),
             pltpu.SemaphoreType.DMA((2,)),
         ],
-        compiler_params=limit(24),
+        compiler_params=limit(16),
         name="first_stage",
     )(at, layer_inputs, out_grads, gain, *pieces)
 
@@ -228,7 +242,7 @@
         out_specs=[VMEM] * 2,
         out_shape=[jax.ShapeDtypeStruct((SEQ, WIDTH), f32), jax.ShapeDtypeStruct((SEQ, QW), bf16)],
         scratch_shapes=[pltpu.VMEM((SEQ, D), bf16), pltpu.SemaphoreType.DMA((1,))],
-        compiler_params=limit(20),
+        compiler_params=limit(10),
         name="more_stage",
     )(at, out_grads, acc, attn_grad, rest, *group)
 
@@ -269,6 +283,8 @@
 
 
 def lane_block(block):
+    if isinstance(block, int):
+        return slice(block * TILE, (block + 1) * TILE)
     return pl.ds(pl.multiple_of(block * TILE, TILE), TILE)
 
 
@@ -436,7 +452,7 @@
             pltpu.VMEM((2 * TILE, D), f32),
             pltpu.SemaphoreType.DMA((2,)),
         ],
-        compiler_params=limit(24),
+        compiler_params=limit(18),
         name="second_stage",
     )(at, layer_inputs, out_grads, gain, *tables, acc, attn_grad, rest, *pieces)
 
@@ -485,7 +501,7 @@
             pltpu.VMEM((TILE, D), f32),
             pltpu.SemaphoreType.DMA((2,)),
         ],
-        compiler_params=limit(24),
+        compiler_params=limit(10),
         name="third_stage",
     )(at, layer_inputs, out_grads, gain, *tables, *carried, *pieces)
 

time: 164 us -> 155 us (0.945)
  local copies, waits for them, and re-layouts: 9.95 us -> 2.53 us
  other arithmetic: 10.4 us -> 4.69 us
  waiting for transfers between devices: 55.5 us -> 60 us
    unnamed x50 -> x22, local copies, waits for them, and re-layouts: 9.95 us -> 2.53 us
    ppermute x27, waiting for transfers between devices: 55.5 us -> 60 us  [passed_along(): lax.ppermute(array, axis, [(i, (i + by) % size) for i in range(size)])]
    convert_element_type x2, other arithmetic: 2.67 us -> 0.41 us  [wide(): return array.astype(f32)]
  transfers between devices with their start and end apart: 27 -> 27, of which waited for: 8 -> 8; matrix products, arithmetic and copies ran while one was open for 6% -> 3% of each run, Pallas kernels for 18% -> 19%
where the time goes in v1:
time: 155 us; the launch traced here: 154 us
  waiting for transfers between devices  60 us (39%)
  Pallas kernels  43.5 us (28%)
  starting transfers between devices  41.4 us (27%)
  other arithmetic  4.69 us (3%)
  local copies, waits for them, and re-layouts  2.53 us (2%)
  between operations  2.19 us (1%)
    ppermute x27, waiting for transfers between devices, passed_along(): lax.ppermute(array, axis, [(i, (i + by) % size) for i in range(size)])  60 us
    ppermute x27, starting transfers between devices, passed_along(): lax.ppermute(array, axis, [(i, (i + by) % size) for i in range(size)])  41.4 us
    pallas_call x1, Pallas kernels, weight_stage(): pl.pallas_call(weight_body, grid_spec=pltpu.PrefetchScalarGridSpec(num_sc...  13.3 us
    pallas_call x1, Pallas kernels, second_stage(): pl.pallas_call(second_body, in_specs=[SMEM, HBM, HBM] + [VMEM] * (6 + 16)...  13 us
    pallas_call x1, Pallas kernels, third_stage(): pl.pallas_call(third_body, in_specs=[SMEM, HBM, HBM] + [VMEM] * (7 + 16),...  6.21 us
    pallas_call x1, Pallas kernels, first_stage(): pl.pallas_call(first_body, in_specs=[SMEM, HBM, HBM] + [VMEM] * (1 + 8),...  5.17 us
  transfers between devices with their start and end apart: 27, of which 8 were waited for; matrix products, arithmetic and copies ran while one was open for 3% of the time, Pallas kernels for 19%

profile of v1, /device:TPU:1, one launch (start us, length us, event | category | flops | bytes accessed | tf_op | source)
XLA Modules:
  0.0 154.3 jit_solution(17566261434675843537)
XLA Ops:
  1.9 13.3 %weight_stage.1 = (bf16[8,640,512]{2,1,0:T(8,128)(2,1)}, bf16[8,640,512]{2,1,0:T(8,128)(2,1)}) custom-call(s32[4]{0:T(128)} %get-tuple-element.31.at, bf16[1,2,384,2048]{3,2,1,0:T(8,128)(2,1)} %x_all.7, bf16[1,2,384,1536]{3,2,1,0:T(8,128)(2,1)} %p_all.1, bf16[1,2,384,1024]{3,2,1,0:T(8,128)(2,1)} %a_all.1, bf16[1,2,384,2048]{3,2,1,0:T(8,128)(2,1)} %e_all.1, ...), custom_call_target="tpu_custom_call" | custom-call | tf_op jit(solution)/shard_map/weight_stage/pallas_call | solution.py:559
  15.2 3.3 %collective-permute-start.17 = (bf16[8,640,512]{2,1,0:T(8,128)(2,1)}, bf16[8,640,512]{2,1,0:T(8,128)(2,1)S(1)}, u32[]{:S(2)}, u32[]{:S(2)}) collective-permute-start(bf16[8,640,512]{2,1,0:T(8,128)(2,1)} %get-tuple-element.28), channel_id=1, source_target_pairs={{0,1},{1,0},{2,3},{3,2},{4,5},{5,4},{6,7},{7,6},{8,9},{9,8},{10,11... | collective-permute-start | bytes 15728648 | tf_op jit(solution)/shard_map/ppermute | solution.py:39
  18.5 1.1 collective-permute-start.1
  20.0 2.7 %collective-permute-start.3 = (bf16[640,512]{1,0:T(8,128)(2,1)S(1)}, bf16[640,512]{1,0:T(8,128)(2,1)S(1)}, u32[]{:S(2)}, u32[]{:S(2)}) collective-permute-start(bf16[640,512]{1,0:T(8,128)(2,1)S(1)} %pack.1.refs_0_), channel_id=1, source_target_pairs={{0,6},{2,0},{4,2},{6,4},{1,7},{3,1},{5,3},{7,5},{8,14},{10,8},{12,... | collective-permute-start | bytes 1966088 | tf_op jit(solution)/shard_map/ppermute | solution.py:39
  22.7 13.7 %collective-permute-done.1.refs_2_ = bf16[640,512]{1,0:T(8,128)(2,1)S(1)} collective-permute-done((bf16[640,512]{1,0:T(8,128)(2,1)S(1)}, bf16[640,512]{1,0:T(8,128)(2,1)S(1)}, u32[]{:S(2)}, u32[]{:S(2)}) %collective-permute-start.1) | collective-permute-done | bytes 655392 | tf_op jit(solution)/shard_map/ppermute | solution.py:39
  37.7 2.1 %collective-permute-done.5.refs_6_ = bf16[640,512]{1,0:T(8,128)(2,1)S(1)} collective-permute-done((bf16[640,512]{1,0:T(8,128)(2,1)S(1)}, bf16[640,512]{1,0:T(8,128)(2,1)S(1)}, u32[]{:S(2)}, u32[]{:S(2)}) %collective-permute-start.5) | collective-permute-done | bytes 655392 | tf_op jit(solution)/shard_map/ppermute | solution.py:39
  39.7 1.3 collective-permute-start.7
  41.1 12.7 %collective-permute-done.9.refs_2_.refs_10_ = bf16[640,512]{1,0:T(8,128)(2,1)S(1)} collective-permute-done((bf16[640,512]{1,0:T(8,128)(2,1)S(1)}, bf16[640,512]{1,0:T(8,128)(2,1)S(1)}, u32[]{:S(2)}, u32[]{:S(2)}) %collective-permute-start.9) | collective-permute-done | bytes 655392 | tf_op jit(solution)/shard_map/ppermute | solution.py:39
  53.7 1.5 collective-permute-start.13
  55.3 2.5 %copy-done.2 = bf16[8,640,512]{2,1,0:T(8,128)(2,1)S(1)} copy-done((bf16[8,640,512]{2,1,0:T(8,128)(2,1)S(1)}, bf16[8,640,512]{2,1,0:T(8,128)(2,1)}, u32[]{:S(2)}) %copy-start.2) | copy-done | bytes 5242904
  58.8 2.7 %collective-permute-start.20 = (bf16[384,512]{1,0:T(8,128)(2,1)S(1)}, bf16[384,512]{1,0:T(8,128)(2,1)S(1)}, u32[]{:S(2)}, u32[]{:S(2)}) collective-permute-start(bf16[384,512]{1,0:T(8,128)(2,1)S(1)} %get-tuple-element.30), channel_id=1, source_target_pairs={{0,6},{2,0},{4,2},{6,4},{1,7},{3,1},{5,3},{7,5},{8,14},{10,8},{12,... | collective-permute-start | bytes 1179656 | tf_op jit(solution)/shard_map/ppermute | solution.py:39
  61.8 2.6 %collective-permute-start.6 = (bf16[640,512]{1,0:T(8,128)(2,1)S(1)}, bf16[640,512]{1,0:T(8,128)(2,1)S(1)}, u32[]{:S(2)}, u32[]{:S(2)}) collective-permute-start(bf16[640,512]{1,0:T(8,128)(2,1)S(1)} %collective-permute-done.5.refs_6_), channel_id=1, source_target_pairs={{0,1},{1,0},{2,3},{3,2},{4,5},{5,4},{6,7},{7,6},{8,9},{9,8},{10,11... | collective-permute-start | bytes 1966088 | tf_op jit(solution)/shard_map/ppermute | solution.py:39
  64.4 4.7 %collective-permute-done.11.refs_12_ = bf16[640,512]{1,0:T(8,128)(2,1)S(1)} collective-permute-done((bf16[640,512]{1,0:T(8,128)(2,1)S(1)}, bf16[640,512]{1,0:T(8,128)(2,1)S(1)}, u32[]{:S(2)}, u32[]{:S(2)}) %collective-permute-start.11) | collective-permute-done | bytes 655392 | tf_op jit(solution)/shard_map/ppermute | solution.py:39
  69.1 3.6 %collective-permute-start.10 = (bf16[640,512]{1,0:T(8,128)(2,1)S(1)}, bf16[640,512]{1,0:T(8,128)(2,1)S(1)}, u32[]{:S(2)}, u32[]{:S(2)}) collective-permute-start(bf16[640,512]{1,0:T(8,128)(2,1)S(1)} %collective-permute-done.9.refs_2_.refs_10_), channel_id=1, source_target_pairs={{0,1},{1,0},{2,3},{3,2},{4,5},{5,4},{6,7},{7,6},{8,9},{9,8},{10,11... | collective-permute-start | bytes 1966088 | tf_op jit(solution)/shard_map/ppermute | solution.py:39
  72.7 1.2 collective-permute-start.8
  74.2 4.1 %collective-permute-done.18 = bf16[384,512]{1,0:T(8,128)(2,1)S(1)} collective-permute-done((bf16[384,512]{1,0:T(8,128)(2,1)S(1)}, bf16[384,512]{1,0:T(8,128)(2,1)S(1)}, u32[]{:S(2)}, u32[]{:S(2)}) %collective-permute-start.18) | collective-permute-done | bytes 393248 | tf_op jit(solution)/shard_map/ppermute | solution.py:39
  78.3 2.2 %collective-permute-start.12 = (bf16[640,512]{1,0:T(8,128)(2,1)S(1)}, bf16[640,512]{1,0:T(8,128)(2,1)S(1)}, u32[]{:S(2)}, u32[]{:S(2)}) collective-permute-start(bf16[640,512]{1,0:T(8,128)(2,1)S(1)} %collective-permute-done.11.refs_12_), channel_id=1, source_target_pairs={{0,1},{1,0},{2,3},{3,2},{4,5},{5,4},{6,7},{7,6},{8,9},{9,8},{10,11... | collective-permute-start | bytes 1966088 | tf_op jit(solution)/shard_map/ppermute | solution.py:39
  81.0 1.9 %collective-permute-start.23 = (bf16[4,256,512]{2,1,0:T(8,128)(2,1)S(1)}, bf16[4,256,512]{2,1,0:T(8,128)(2,1)S(1)}, u32[]{:S(2)}, u32[]{:S(2)}) collective-permute-start(bf16[4,256,512]{2,1,0:T(8,128)(2,1)S(1)} %add_convert_fusion), channel_id=1, source_target_pairs={{0,8},{8,0},{1,9},{9,1},{2,10},{10,2},{3,11},{11,3},{4,12},{12,4},... | collective-permute-start | bytes 3145736 | tf_op jit(solution)/shard_map/ppermute | solution.py:39
  83.0 1.5 collective-permute-start.19
  85.5 5.2 %first_stage.1 = (f32[384,1536]{1,0:T(8,128)S(1)}, bf16[384,1024]{1,0:T(8,128)(2,1)S(1)}, bf16[384,1024]{1,0:T(8,128)(2,1)S(1)}) custom-call(s32[4]{0:T(128)S(1)} %pad_add_fusion.at, bf16[1,2,384,2048]{3,2,1,0:T(8,128)(2,1)S(1)} %copy-done.1, bf16[1,2,384,2048]{3,2,1,0:T(8,128)(2,1)S(1)} %copy-done, f32[1,2048]{1,0:T(1,128)S(1)} %copy-done.6, ...), custom_call_target="tpu_custom_call" | custom-call | tf_op jit(solution)/shard_map/first_stage/pallas_call | solution.py:207
  90.7 3.0 %more_stage.1 = (f32[384,1536]{1,0:T(8,128)S(1)}, bf16[384,1024]{1,0:T(8,128)(2,1)S(1)}) custom-call(s32[4]{0:T(128)S(1)} %pad_add_fusion.at, bf16[1,2,384,2048]{3,2,1,0:T(8,128)(2,1)S(1)} %copy-done, f32[384,1536]{1,0:T(8,128)S(1)} %get-tuple-element.17.acc_in, bf16[384,1024]{1,0:T(8,128)(2,1)S(1)} %get-tuple-element.18.attn_in, ...), custom_call_target="tpu_custom_call" | custom-call | tf_op jit(solution)/shard_map/more_stage/pallas_call | solution.py:239
  93.7 13.0 %second_stage.1 = (bf16[256,2048]{1,0:T(8,128)(2,1)S(1)}, bf16[128,1536]{1,0:T(8,128)(2,1)S(1)}, bf16[128,1024]{1,0:T(8,128)(2,1)S(1)}, f32[4,128,128]{2,1,0:T(8,128)S(1)}, f32[4,128,128]{2,1,0:T(8,128)S(1)}) custom-call(s32[4]{0:T(128)S(1)} %pad_add_fusion.at, bf16[1,2,384,2048]{3,2,1,0:T(8,128)(2,1)S(1)} %copy-done.1, ...), custom_call_target="tpu_custom_call" | custom-call | tf_op jit(solution)/shard_map/second_stage/pallas_call | solution.py:432
  106.7 5.9 %collective-permute-start.16 = (bf16[256,2048]{1,0:T(8,128)(2,1)S(1)}, bf16[256,2048]{1,0:T(8,128)(2,1)S(1)}, u32[]{:S(2)}, u32[]{:S(2)}) collective-permute-start(bf16[256,2048]{1,0:T(8,128)(2,1)S(1)} %get-tuple-element.26), channel_id=1, source_target_pairs={{0,240},{16,0},{32,16},{48,32},{64,48},{80,64},{96,80},{112,96},{1... | collective-permute-start | bytes 3145736 | tf_op jit(solution)/shard_map/ppermute | solution.py:39
  112.7 6.2 %third_stage.1 = bf16[128,2048]{1,0:T(8,128)(2,1)S(1)} custom-call(s32[4]{0:T(128)S(1)} %pad_add_fusion.at, bf16[1,2,384,2048]{3,2,1,0:T(8,128)(2,1)S(1)} %copy-done.1, bf16[1,2,384,2048]{3,2,1,0:T(8,128)(2,1)S(1)} %copy-done, f32[1,2048]{1,0:T(1,128)S(1)} %copy-done.6, f32[384,128]{1,0:T(8,128)S(1)} %get-tuple-element.45.cosine, ...), custom_call_target="tpu_custom_call" | custom-call | tf_op jit(solution)/shard_map/third_stage/pallas_call | solution.py:490
  118.9 1.2 collective-permute-start.15
  121.1 1.3 collective-permute-start.22
  122.8 1.4 collective-permute-start.24
  124.3 1.8 %collective-permute-start.25 = (bf16[256,512]{1,0:T(8,128)(2,1)S(1)}, bf16[256,512]{1,0:T(8,128)(2,1)S(1)}, u32[]{:S(2)}, u32[]{:S(2)}) collective-permute-start(bf16[256,512]{1,0:T(8,128)(2,1)S(1)} %get-tuple-element.36), channel_id=1, source_target_pairs={{0,2},{2,4},{4,6},{6,0},{1,3},{3,5},{5,7},{7,1},{8,10},{10,12},{12... | collective-permute-start | bytes 786440 | tf_op jit(solution)/shard_map/ppermute | solution.py:39
  126.1 19.0 %collective-permute-done.15 = bf16[128,2048]{1,0:T(8,128)(2,1)S(1)} collective-permute-done((bf16[128,2048]{1,0:T(8,128)(2,1)S(1)}, bf16[128,2048]{1,0:T(8,128)(2,1)S(1)}, u32[]{:S(2)}, u32[]{:S(2)}) %collective-permute-start.15) | collective-permute-done | bytes 524320 | tf_op jit(solution)/shard_map/ppermute | solution.py:39
  145.1 2.5 %collective-permute-start.26 = (bf16[256,512]{1,0:T(8,128)(2,1)S(1)}, bf16[256,512]{1,0:T(8,128)(2,1)S(1)}, u32[]{:S(2)}, u32[]{:S(2)}) collective-permute-start(bf16[256,512]{1,0:T(8,128)(2,1)S(1)} %get-tuple-element.35), channel_id=1, source_target_pairs={{0,6},{2,0},{4,2},{6,4},{1,7},{3,1},{5,3},{7,5},{8,14},{10,8},{12,... | collective-permute-start | bytes 786440 | tf_op jit(solution)/shard_map/ppermute | solution.py:39
  147.6 1.2 maximum_bitcast_fusion
  148.8 2.7 %collective-permute-done.26.below = bf16[256,512]{1,0:T(8,128)(2,1)S(1)} collective-permute-done((bf16[256,512]{1,0:T(8,128)(2,1)S(1)}, bf16[256,512]{1,0:T(8,128)(2,1)S(1)}, u32[]{:S(2)}, u32[]{:S(2)}) %collective-permute-start.26) | collective-permute-done | bytes 262176 | tf_op jit(solution)/shard_map/ppermute | solution.py:39
  (67 shorter events, 9.0 us)
Async XLA Ops:
  1.9 16.6 %copy-start.5 = (bf16[1,64,2048]{2,1,0:T(8,128)(2,1)S(1)}, bf16[1,64,2048]{2,1,0:T(8,128)(2,1)}, u32[]{:S(2)}) copy-start(bf16[1,64,2048]{2,1,0:T(8,128)(2,1)} %out.1) | copy-start | bytes 786436
  1.9 53.3 %copy-start.7 = (f32[24,32]{1,0:T(8,128)S(1)}, f32[24,32]{1,0:T(8,128)}, u32[]{:S(2)}) copy-start(f32[24,32]{1,0:T(8,128)} %constant.21.clone) | copy-start | bytes 9220
  1.9 53.3 %copy-start.8 = (f32[24,32]{1,0:T(8,128)S(1)}, f32[24,32]{1,0:T(8,128)}, u32[]{:S(2)}) copy-start(f32[24,32]{1,0:T(8,128)} %constant.19.clone) | copy-start | bytes 9220
  1.9 53.3 %copy-start.9 = (f32[16,32]{1,0:T(8,128)S(1)}, f32[16,32]{1,0:T(8,128)}, u32[]{:S(2)}) copy-start(f32[16,32]{1,0:T(8,128)} %constant.22.clone) | copy-start | bytes 6148
  1.9 53.3 %copy-start.10 = (f32[16,32]{1,0:T(8,128)S(1)}, f32[16,32]{1,0:T(8,128)}, u32[]{:S(2)}) copy-start(f32[16,32]{1,0:T(8,128)} %constant.20.clone) | copy-start | bytes 6148
  15.2 38.5 %collective-permute-start.17 = (bf16[8,640,512]{2,1,0:T(8,128)(2,1)}, bf16[8,640,512]{2,1,0:T(8,128)(2,1)S(1)}, u32[]{:S(2)}, u32[]{:S(2)}) collective-permute-start(bf16[8,640,512]{2,1,0:T(8,128)(2,1)} %get-tuple-element.28), channel_id=1, source_target_pairs={{0,1},{1,0},{2,3},{3,2},{4,5},{5,4},{6,7},{7,6},{8,9},{9,8},{10,11... | collective-permute-start | bytes 15728648 | tf_op jit(solution)/shard_map/ppermute | solution.py:39
  18.5 17.9 %collective-permute-start.1 = (bf16[640,512]{1,0:T(8,128)(2,1)S(1)}, bf16[640,512]{1,0:T(8,128)(2,1)S(1)}, u32[]{:S(2)}, u32[]{:S(2)}) collective-permute-start(bf16[640,512]{1,0:T(8,128)(2,1)S(1)} %pack.1.refs_0_), channel_id=1, source_target_pairs={{0,8},{8,0},{1,9},{9,1},{2,10},{10,2},{3,11},{11,3},{4,12},{12,4},... | collective-permute-start | bytes 1966088 | tf_op jit(solution)/shard_map/ppermute | solution.py:39
  19.7 16.7 %collective-permute-start = (bf16[640,512]{1,0:T(8,128)(2,1)S(1)}, bf16[640,512]{1,0:T(8,128)(2,1)S(1)}, u32[]{:S(2)}, u32[]{:S(2)}) collective-permute-start(bf16[640,512]{1,0:T(8,128)(2,1)S(1)} %pack.1.refs_0_), channel_id=1, source_target_pairs={{0,1},{1,0},{2,3},{3,2},{4,5},{5,4},{6,7},{7,6},{8,9},{9,8},{10,11... | collective-permute-start | bytes 1966088 | tf_op jit(solution)/shard_map/ppermute | solution.py:39
  20.0 17.3 %collective-permute-start.3 = (bf16[640,512]{1,0:T(8,128)(2,1)S(1)}, bf16[640,512]{1,0:T(8,128)(2,1)S(1)}, u32[]{:S(2)}, u32[]{:S(2)}) collective-permute-start(bf16[640,512]{1,0:T(8,128)(2,1)S(1)} %pack.1.refs_0_), channel_id=1, source_target_pairs={{0,6},{2,0},{4,2},{6,4},{1,7},{3,1},{5,3},{7,5},{8,14},{10,8},{12,... | collective-permute-start | bytes 1966088 | tf_op jit(solution)/shard_map/ppermute | solution.py:39
  22.7 17.0 %collective-permute-start.5 = (bf16[640,512]{1,0:T(8,128)(2,1)S(1)}, bf16[640,512]{1,0:T(8,128)(2,1)S(1)}, u32[]{:S(2)}, u32[]{:S(2)}) collective-permute-start(bf16[640,512]{1,0:T(8,128)(2,1)S(1)} %pack.1.refs_0_), channel_id=1, source_target_pairs={{0,2},{2,4},{4,6},{6,0},{1,3},{3,5},{5,7},{7,1},{8,10},{10,12},{12... | collective-permute-start | bytes 1966088 | tf_op jit(solution)/shard_map/ppermute | solution.py:39
  36.4 17.4 %collective-permute-start.9 = (bf16[640,512]{1,0:T(8,128)(2,1)S(1)}, bf16[640,512]{1,0:T(8,128)(2,1)S(1)}, u32[]{:S(2)}, u32[]{:S(2)}) collective-permute-start(bf16[640,512]{1,0:T(8,128)(2,1)S(1)} %collective-permute-done.1.refs_2_), channel_id=1, source_target_pairs={{0,2},{2,4},{4,6},{6,0},{1,3},{3,5},{5,7},{7,1},{8,10},{10,12},{12... | collective-permute-start | bytes 1966088 | tf_op jit(solution)/shard_map/ppermute | solution.py:39
  36.4 22.3 %collective-permute-start.2 = (bf16[640,512]{1,0:T(8,128)(2,1)S(1)}, bf16[640,512]{1,0:T(8,128)(2,1)S(1)}, u32[]{:S(2)}, u32[]{:S(2)}) collective-permute-start(bf16[640,512]{1,0:T(8,128)(2,1)S(1)} %collective-permute-done.1.refs_2_), channel_id=1, source_target_pairs={{0,1},{1,0},{2,3},{3,2},{4,5},{5,4},{6,7},{7,6},{8,9},{9,8},{10,11... | collective-permute-start | bytes 1966088 | tf_op jit(solution)/shard_map/ppermute | solution.py:39
  37.3 21.6 %collective-permute-start.4 = (bf16[640,512]{1,0:T(8,128)(2,1)S(1)}, bf16[640,512]{1,0:T(8,128)(2,1)S(1)}, u32[]{:S(2)}, u32[]{:S(2)}) collective-permute-start(bf16[640,512]{1,0:T(8,128)(2,1)S(1)} %collective-permute-done.3.refs_4_), channel_id=1, source_target_pairs={{0,1},{1,0},{2,3},{3,2},{4,5},{5,4},{6,7},{7,6},{8,9},{9,8},{10,11... | collective-permute-start | bytes 1966088 | tf_op jit(solution)/shard_map/ppermute | solution.py:39
  39.7 22.1 %collective-permute-start.7 = (bf16[640,512]{1,0:T(8,128)(2,1)S(1)}, bf16[640,512]{1,0:T(8,128)(2,1)S(1)}, u32[]{:S(2)}, u32[]{:S(2)}) collective-permute-start(bf16[640,512]{1,0:T(8,128)(2,1)S(1)} %collective-permute-done.1.refs_2_), channel_id=1, source_target_pairs={{0,6},{2,0},{4,2},{6,4},{1,7},{3,1},{5,3},{7,5},{8,14},{10,8},{12,... | collective-permute-start | bytes 1966088 | tf_op jit(solution)/shard_map/ppermute | solution.py:39
  53.7 15.4 %collective-permute-start.11 = (bf16[640,512]{1,0:T(8,128)(2,1)S(1)}, bf16[640,512]{1,0:T(8,128)(2,1)S(1)}, u32[]{:S(2)}, u32[]{:S(2)}) collective-permute-start(bf16[640,512]{1,0:T(8,128)(2,1)S(1)} %collective-permute-done.3.refs_4_), channel_id=1, source_target_pairs={{0,6},{2,0},{4,2},{6,4},{1,7},{3,1},{5,3},{7,5},{8,14},{10,8},{12,... | collective-permute-start | bytes 1966088 | tf_op jit(solution)/shard_map/ppermute | solution.py:39
  53.7 19.0 %collective-permute-start.13 = (bf16[640,512]{1,0:T(8,128)(2,1)S(1)}, bf16[640,512]{1,0:T(8,128)(2,1)S(1)}, u32[]{:S(2)}, u32[]{:S(2)}) collective-permute-start(bf16[640,512]{1,0:T(8,128)(2,1)S(1)} %collective-permute-done.9.refs_2_.refs_10_), channel_id=1, source_target_pairs={{0,2},{2,4},{4,6},{6,0},{1,3},{3,5},{5,7},{7,1},{8,10},{10,12},{12... | collective-permute-start | bytes 1966088 | tf_op jit(solution)/shard_map/ppermute | solution.py:39
  58.7 19.6 %collective-permute-start.18 = (bf16[384,512]{1,0:T(8,128)(2,1)S(1)}, bf16[384,512]{1,0:T(8,128)(2,1)S(1)}, u32[]{:S(2)}, u32[]{:S(2)}) collective-permute-start(bf16[384,512]{1,0:T(8,128)(2,1)S(1)} %get-tuple-element.29), channel_id=1, source_target_pairs={{0,2},{2,4},{4,6},{6,0},{1,3},{3,5},{5,7},{7,1},{8,10},{10,12},{12... | collective-permute-start | bytes 1179656 | tf_op jit(solution)/shard_map/ppermute | solution.py:39
  58.8 21.7 %collective-permute-start.20 = (bf16[384,512]{1,0:T(8,128)(2,1)S(1)}, bf16[384,512]{1,0:T(8,128)(2,1)S(1)}, u32[]{:S(2)}, u32[]{:S(2)}) collective-permute-start(bf16[384,512]{1,0:T(8,128)(2,1)S(1)} %get-tuple-element.30), channel_id=1, source_target_pairs={{0,6},{2,0},{4,2},{6,4},{1,7},{3,1},{5,3},{7,5},{8,14},{10,8},{12,... | collective-permute-start | bytes 1179656 | tf_op jit(solution)/shard_map/ppermute | solution.py:39
  61.8 19.2 %collective-permute-start.6 = (bf16[640,512]{1,0:T(8,128)(2,1)S(1)}, bf16[640,512]{1,0:T(8,128)(2,1)S(1)}, u32[]{:S(2)}, u32[]{:S(2)}) collective-permute-start(bf16[640,512]{1,0:T(8,128)(2,1)S(1)} %collective-permute-done.5.refs_6_), channel_id=1, source_target_pairs={{0,1},{1,0},{2,3},{3,2},{4,5},{5,4},{6,7},{7,6},{8,9},{9,8},{10,11... | collective-permute-start | bytes 1966088 | tf_op jit(solution)/shard_map/ppermute | solution.py:39
  69.1 13.8 %collective-permute-start.10 = (bf16[640,512]{1,0:T(8,128)(2,1)S(1)}, bf16[640,512]{1,0:T(8,128)(2,1)S(1)}, u32[]{:S(2)}, u32[]{:S(2)}) collective-permute-start(bf16[640,512]{1,0:T(8,128)(2,1)S(1)} %collective-permute-done.9.refs_2_.refs_10_), channel_id=1, source_target_pairs={{0,1},{1,0},{2,3},{3,2},{4,5},{5,4},{6,7},{7,6},{8,9},{9,8},{10,11... | collective-permute-start | bytes 1966088 | tf_op jit(solution)/shard_map/ppermute | solution.py:39
  72.7 10.2 %collective-permute-start.8 = (bf16[640,512]{1,0:T(8,128)(2,1)S(1)}, bf16[640,512]{1,0:T(8,128)(2,1)S(1)}, u32[]{:S(2)}, u32[]{:S(2)}) collective-permute-start(bf16[640,512]{1,0:T(8,128)(2,1)S(1)} %collective-permute-done.7.refs_0_.refs_8_), channel_id=1, source_target_pairs={{0,1},{1,0},{2,3},{3,2},{4,5},{5,4},{6,7},{7,6},{8,9},{9,8},{10,11... | collective-permute-start | bytes 1966088 | tf_op jit(solution)/shard_map/ppermute | solution.py:39
  78.3 15.4 %collective-permute-start.12 = (bf16[640,512]{1,0:T(8,128)(2,1)S(1)}, bf16[640,512]{1,0:T(8,128)(2,1)S(1)}, u32[]{:S(2)}, u32[]{:S(2)}) collective-permute-start(bf16[640,512]{1,0:T(8,128)(2,1)S(1)} %collective-permute-done.11.refs_12_), channel_id=1, source_target_pairs={{0,1},{1,0},{2,3},{3,2},{4,5},{5,4},{6,7},{7,6},{8,9},{9,8},{10,11... | collective-permute-start | bytes 1966088 | tf_op jit(solution)/shard_map/ppermute | solution.py:39
  80.5 13.2 %collective-permute-start.14 = (bf16[640,512]{1,0:T(8,128)(2,1)S(1)}, bf16[640,512]{1,0:T(8,128)(2,1)S(1)}, u32[]{:S(2)}, u32[]{:S(2)}) collective-permute-start(bf16[640,512]{1,0:T(8,128)(2,1)S(1)} %collective-permute-done.13.refs_14_), channel_id=1, source_target_pairs={{0,1},{1,0},{2,3},{3,2},{4,5},{5,4},{6,7},{7,6},{8,9},{9,8},{10,11... | collective-permute-start | bytes 1966088 | tf_op jit(solution)/shard_map/ppermute | solution.py:39
  81.0 41.3 %collective-permute-start.23 = (bf16[4,256,512]{2,1,0:T(8,128)(2,1)S(1)}, bf16[4,256,512]{2,1,0:T(8,128)(2,1)S(1)}, u32[]{:S(2)}, u32[]{:S(2)}) collective-permute-start(bf16[4,256,512]{2,1,0:T(8,128)(2,1)S(1)} %add_convert_fusion), channel_id=1, source_target_pairs={{0,8},{8,0},{1,9},{9,1},{2,10},{10,2},{3,11},{11,3},{4,12},{12,4},... | collective-permute-start | bytes 3145736 | tf_op jit(solution)/shard_map/ppermute | solution.py:39
  82.9 37.2 %collective-permute-start.21 = (bf16[768,512]{1,0:T(8,128)(2,1)S(1)}, bf16[768,512]{1,0:T(8,128)(2,1)S(1)}, u32[]{:S(2)}, u32[]{:S(2)}) collective-permute-start(bf16[768,512]{1,0:T(8,128)(2,1)S(1)} %pad_maximum_fusion.1), channel_id=1, source_target_pairs={{0,6},{2,0},{4,2},{6,4},{1,7},{3,1},{5,3},{7,5},{8,14},{10,8},{12,... | collective-permute-start | bytes 2359304 | tf_op jit(solution)/shard_map/ppermute | solution.py:39
  83.0 37.4 %collective-permute-start.19 = (bf16[768,512]{1,0:T(8,128)(2,1)S(1)}, bf16[768,512]{1,0:T(8,128)(2,1)S(1)}, u32[]{:S(2)}, u32[]{:S(2)}) collective-permute-start(bf16[768,512]{1,0:T(8,128)(2,1)S(1)} %pad_maximum_fusion), channel_id=1, source_target_pairs={{0,2},{2,4},{4,6},{6,0},{1,3},{3,5},{5,7},{7,1},{8,10},{10,12},{12... | collective-permute-start | bytes 2359304 | tf_op jit(solution)/shard_map/ppermute | solution.py:39
  106.7 40.8 %collective-permute-start.16 = (bf16[256,2048]{1,0:T(8,128)(2,1)S(1)}, bf16[256,2048]{1,0:T(8,128)(2,1)S(1)}, u32[]{:S(2)}, u32[]{:S(2)}) collective-permute-start(bf16[256,2048]{1,0:T(8,128)(2,1)S(1)} %get-tuple-element.26), channel_id=1, source_target_pairs={{0,240},{16,0},{32,16},{48,32},{64,48},{80,64},{96,80},{112,96},{1... | collective-permute-start | bytes 3145736 | tf_op jit(solution)/shard_map/ppermute | solution.py:39
  118.9 26.2 %collective-permute-start.15 = (bf16[128,2048]{1,0:T(8,128)(2,1)S(1)}, bf16[128,2048]{1,0:T(8,128)(2,1)S(1)}, u32[]{:S(2)}, u32[]{:S(2)}) collective-permute-start(bf16[128,2048]{1,0:T(8,128)(2,1)S(1)} %third_stage.1), channel_id=1, source_target_pairs={{0,240},{16,0},{32,16},{48,32},{64,48},{80,64},{96,80},{112,96},{1... | collective-permute-start | bytes 1572872 | tf_op jit(solution)/shard_map/ppermute | solution.py:39
  121.1 32.3 %collective-permute-start.22 = (bf16[384,512]{1,0:T(8,128)(2,1)S(1)}, bf16[384,512]{1,0:T(8,128)(2,1)S(1)}, u32[]{:S(2)}, u32[]{:S(2)}) collective-permute-start(bf16[384,512]{1,0:T(8,128)(2,1)S(1)} %get-tuple-element.33), channel_id=1, source_target_pairs={{0,8},{8,0},{1,9},{9,1},{2,10},{10,2},{3,11},{11,3},{4,12},{12,4},... | collective-permute-start | bytes 1179656 | tf_op jit(solution)/shard_map/ppermute | solution.py:39
  122.8 26.0 %collective-permute-start.24 = (bf16[256,512]{1,0:T(8,128)(2,1)S(1)}, bf16[256,512]{1,0:T(8,128)(2,1)S(1)}, u32[]{:S(2)}, u32[]{:S(2)}) collective-permute-start(bf16[256,512]{1,0:T(8,128)(2,1)S(1)} %get-tuple-element.37), channel_id=1, source_target_pairs={{0,4},{2,6},{4,0},{6,2},{1,5},{3,7},{5,1},{7,3},{8,12},{10,14},{12... | collective-permute-start | bytes 786440 | tf_op jit(solution)/shard_map/ppermute | solution.py:39
  124.3 24.6 %collective-permute-start.25 = (bf16[256,512]{1,0:T(8,128)(2,1)S(1)}, bf16[256,512]{1,0:T(8,128)(2,1)S(1)}, u32[]{:S(2)}, u32[]{:S(2)}) collective-permute-start(bf16[256,512]{1,0:T(8,128)(2,1)S(1)} %get-tuple-element.36), channel_id=1, source_target_pairs={{0,2},{2,4},{4,6},{6,0},{1,3},{3,5},{5,7},{7,1},{8,10},{10,12},{12... | collective-permute-start | bytes 786440 | tf_op jit(solution)/shard_map/ppermute | solution.py:39
  145.1 6.4 %collective-permute-start.26 = (bf16[256,512]{1,0:T(8,128)(2,1)S(1)}, bf16[256,512]{1,0:T(8,128)(2,1)S(1)}, u32[]{:S(2)}, u32[]{:S(2)}) collective-permute-start(bf16[256,512]{1,0:T(8,128)(2,1)S(1)} %get-tuple-element.35), channel_id=1, source_target_pairs={{0,6},{2,0},{4,2},{6,4},{1,7},{3,1},{5,3},{7,5},{8,14},{10,8},{12,... | collective-permute-start | bytes 786440 | tf_op jit(solution)/shard_map/ppermute | solution.py:39
  (6 other events, 37.1 us)
